TPU v7x, 256 devices: a whole 4x4x8 slice. The times are simulated.
256 devices in a mesh: prow: 32 (over x, z), pcol: 8 (over y, core).
Axes of the slice: x: 4, y: 4, z: 8, core: 2. Of those that a mesh axis runs over, the one named last changes fastest.
Arguments:
- inverse_pool: float32 [12288, 12288], P('prow', 'pcol'), may hold values from -6 to 6
- panel_one: float32 [12288, 512], P(('prow', 'pcol')), may hold values from -0.0625 to 0.0625
- panel_two: float32 [12288, 512], P(('prow', 'pcol')), may hold values from -0.078125 to 0.078125
- upper_two: float32 [512, 512], replicated, may hold values from -0.25 to 0.25
- lower_one: float32 [512, 512], replicated, as said below
- lower_two: float32 [512, 512], replicated, as said below
- list_one: int32 [72], replicated, may hold values from 0 to 95, as said below
- list_two: int32 [48], replicated, may hold values from 0 to 95, as said below
Outputs:
- first_offdiag: float32 [12288, 512], P(('prow', 'pcol'))
- first_diag: float32 [512, 512], replicated
- second_offdiag: float32 [12288, 512], P(('prow', 'pcol'))
- second_coupling: float32 [512, 512], replicated
- second_diag: float32 [512, 512], replicated
Inputs may be any that keep to these rules, and one draw needn't show every extreme that they name: `list_one`: distinct block numbers, among them 0, 48 and 95. `list_two`: distinct block numbers, each of which is also in list_one, among them 0, 48 and 95. `lower_one`: lower triangular with a diagonal of 1 to 1.5. `lower_two`: lower triangular with a diagonal of 1 to 1.5.
All inputs are finite; a program needn't handle non-finite values.
Results may differ from a plain program's by a relative error of at most 0.000073.
Values sent between devices are 32-bit elements; how exact they have to be, the bound alone decides.
No kernel may reach another device: no remote copies, remote signals or barrier semaphores. Data moves between devices by JAX's collectives and lax.ppermute only.
A program may use at most 64 MiB of HBM per device.

v0:
```python
import jax
import jax.numpy as jnp
from jax import lax
from jax.experimental import pallas as pl
from jax.experimental.pallas import tpu as pltpu
from jax.sharding import Mesh
from jax.sharding import PartitionSpec as P


BLK = 128
LEAD = 2
SIZES = {"x": 4, "z": 8, "y": 4, "k": 2}
ALL = ("x", "z", "y", "k")
F32 = jnp.float32
BF16 = jnp.bfloat16


def call(body, out_shapes, *args, scratch=()):
    whole = pl.BlockSpec(memory_space=pltpu.VMEM)
    return pl.pallas_call(
        body,
        out_shape=out_shapes,
        in_specs=[whole] * len(args),
        out_specs=jax.tree.map(lambda _: whole, out_shapes),
        scratch_shapes=list(scratch),
    )(*args)


def arr(*shape, dtype=F32):
    return jax.ShapeDtypeStruct(shape, dtype)


def halves(v):
    hi = v.astype(BF16)
    return hi, (v - hi.astype(F32)).astype(BF16)


def dot3(a, b, dims):
    def one(l, r):
        return lax.dot_general(l, r, (dims, ((), ())), preferred_element_type=F32)

    return one(a[0], b[0]) + (one(a[0], b[1]) + one(a[1], b[0]))


def shifted(v, axis, by):
    n = SIZES[axis]
    return lax.ppermute(v, axis, [(i, (i + by) % n) for i in range(n)])


def crossed(v, axis, mask):
    return lax.ppermute(v, axis, [(i, i ^ mask) for i in range(SIZES[axis])])


def traded(v, axis):
    return lax.all_to_all(v, axis, split_axis=0, concat_axis=0, tiled=True)


def spread(v, axis):
    return [v] + [shifted(v, axis, d) for d in range(1, SIZES[axis])]


def place(axis, d, step):
    n = SIZES[axis]
    return pl.multiple_of(lax.rem(lax.axis_index(axis) + (n + d) % n, n) * step, step)


def masks(list_one, list_two, panel_one, panel_two):
    rows, cols = panel_one.shape

    def body(one_list, two_list, one, two, both, out1, out2, keep1, keep2):
        index = lax.axis_index("x")
        for axis in ("z", "y", "k"):
            index = index * SIZES[axis] + lax.axis_index(axis)
        for listing, panel, out, keep, at in ((one_list, one, out1, keep1, 0), (two_list, two, out2, keep2, cols)):
            row = lax.broadcasted_iota(jnp.int32, (rows, listing.shape[1]), 0) + index * rows
            hits = jnp.where(lax.shift_right_logical(row, 7) == listing[...], 1.0, 0.0).astype(F32)
            live = jnp.max(hits, axis=1, keepdims=True)
            keep[...] = jnp.broadcast_to(live, (rows, BLK))
            v = live * panel[...]
            out[...] = v
            both[:, at : at + cols] = v

    shapes = [arr(rows, 2 * cols)] + [arr(rows, cols)] * 2 + [arr(rows, BLK)] * 2
    return call(body, shapes, list_one[None], list_two[None], panel_one, panel_two)


def split_tile(tile, span):
    rows, cols = tile.shape
    n = rows // (2 * span)

    def body(a, hi, lo):
        k = lax.axis_index("k")
        for half, core in ((0, k), (1, 1 - k)):
            for b in range(n):
                v = a[pl.ds(pl.multiple_of((2 * b + core) * span, span), span), :]
                h, l = halves(v)
                at = half * (rows // 2) + b * span
                hi[at : at + span, :] = h
                lo[at : at + span, :] = l

    return call(body, [arr(rows, cols, dtype=BF16)] * 2, tile)


def stacked(pieces, axis, cuts):
    n = SIZES[axis]
    rows, cols = pieces[0].shape
    width = cols // cuts

    def body(*refs):
        for d in range(n):
            for c in range(cuts):
                at = pl.ds(place(axis, -d, rows), rows)
                refs[n + c][at, :] = refs[d][:, c * width : (c + 1) * width]

    return call(body, [arr(n * rows, width)] * cuts, *pieces)


def stacked_halves(pieces, axis):
    n = SIZES[axis]
    rows, cols = pieces[0].shape

    def body(*refs):
        whole = refs[-1]
        for d in range(n):
            whole[pl.ds(place(axis, -d, rows), rows), :] = refs[d][...]
        refs[n][...] = whole[: n * rows // 2]
        refs[n + 1][...] = whole[n * rows // 2 :]

    return call(body, [arr(n * rows // 2, cols)] * 2, *pieces, scratch=[pltpu.VMEM((n * rows, cols), F32)])


def spot(x, z):
    order = lax.rem(z + 10 - 4 * lax.axis_index("k"), 8)
    turn = lax.rem(x + 4 - lax.axis_index("y"), 4)
    side = jnp.where(turn == 0, 1, jnp.where(turn == 1, 4, jnp.where(turn == 2, 0, 5)))
    return lax.shift_right_logical(order, 1) * 8 + lax.rem(order, 2) * 2 + side


def multiply(tile_hi, tile_lo, chunks, cols, span):
    rows, depth = tile_hi.shape
    m = len(chunks)
    wide = 256

    def body(*refs):
        hi, lo = refs[0], refs[1]
        keep, send, b_hi, b_lo = refs[2 + m :]
        for ref, (_, column, at_of) in zip(refs[2 : 2 + m], chunks):
            for b in range(ref.shape[0] // span):
                h, l = halves(ref[b * span : (b + 1) * span, :])
                at = pl.ds(pl.multiple_of(spot(*at_of(b)) * span, span), span)
                b_hi[at, column : column + ref.shape[1]] = h
                b_lo[at, column : column + ref.shape[1]] = l

        def step(i, carry):
            at = pl.ds(pl.multiple_of(i * wide, wide), wide)
            v = dot3((hi[...], lo[...]), (b_hi[:, at], b_lo[:, at]), ((1,), (0,)))
            keep[:, at] = v[: rows // 2]
            send[:, at] = v[rows // 2 :]
            return carry

        lax.fori_loop(0, cols // wide, step, 0)

    return call(
        body,
        [arr(rows // 2, cols)] * 2,
        tile_hi,
        tile_lo,
        *[c[0] for c in chunks],
        scratch=[pltpu.VMEM((depth, cols), BF16)] * 2,
    )


def by_column(keep_one, came_one, keep_two, came_two):
    rows, cols = keep_one.shape
    n = cols // BLK

    def body(k1, c1, k2, c2, out):
        for i in range(n):
            at = slice(i * BLK, (i + 1) * BLK)
            out[i, :, :BLK] = k1[:, at] + c1[:, at]
            out[i, :, BLK:] = k2[:, at] + c2[:, at]

    return call(body, arr(n, rows, 2 * BLK), keep_one, came_one, keep_two, came_two)


def contract(parts, beside):
    n, rows, cols = parts.shape
    span, depth = beside[0].shape
    width = depth // 2
    half = 3 * width // 2

    def body(ins, *refs):
        total, keep, send, terms, left = refs[n:]
        for d in range(n):
            left[pl.ds(place("y", -d, span), span), :] = refs[d][...]
        v = ins[0]
        for i in range(1, n):
            v = v + ins[i]
        total[...] = v
        one = halves(v[:, :BLK])
        two = halves(v[:, BLK:])
        terms[: 2 * width, :] = dot3(halves(left[...]), one, ((0,), (0,)))
        terms[2 * width :, :] = dot3(halves(left[:, width:]), two, ((0,), (0,)))
        k = lax.axis_index("k")
        keep[...] = terms[pl.ds(pl.multiple_of(k * half, half), half), :]
        send[...] = terms[pl.ds(pl.multiple_of((1 - k) * half, half), half), :]

    shapes = [arr(rows, cols)] + [arr(half, BLK)] * 2
    return call(
        body, shapes, parts, *beside, scratch=[pltpu.VMEM((2 * half, BLK), F32), pltpu.VMEM((rows, depth), F32)]
    )


def in_columns(cols, wide, body):
    def step(i, carry):
        body(pl.ds(pl.multiple_of(i * wide, wide), wide))
        return carry

    lax.fori_loop(0, cols // wide, step, 0)


def gram(lower):
    side = lower.shape[0]

    def body(ref, out):
        whole = halves(ref[...])

        def part(at):
            out[:, at] = dot3(whole, halves(ref[:, at]), ((0,), (0,)))

        in_columns(side, 256, part)

    return call(body, arr(side, side), lower)


def finish(mine, other, gram_one, gram_two, upper):
    _, rows, cols = mine.shape
    side = upper.shape[0]
    half = rows * 4

    def body(own, far, g1, g2, u_ref, d1_ref, c_ref, d2_ref, terms):
        k = lax.axis_index("k")
        for ref, core in ((own, k), (far, 1 - k)):
            for x in range(4):
                at = pl.ds(pl.multiple_of(core * half + x * rows, rows), rows)
                for y in range(4):
                    terms[at, y * cols : (y + 1) * cols] = ref[4 * x + y]
        d1_ref[...] = g1[...] + terms[:side, :]
        c_ref[...] = terms[side : 2 * side, :].T

        def coupling(at):
            c_ref[:, at] = c_ref[:, at] - dot3(halves(d1_ref[...]), halves(u_ref[:, at]), ((1,), (0,)))

        def last(at):
            cross = halves(terms[side : 2 * side, :])
            d2_ref[:, at] = (
                g2[:, at]
                + terms[2 * side :, at]
                - dot3(cross, halves(u_ref[:, at]), ((1,), (0,)))
                - dot3(halves(u_ref[...]), halves(c_ref[:, at]), ((0,), (0,)))
            )

        in_columns(side, 256, coupling)
        in_columns(side, 256, last)

    return call(
        body,
        [arr(side, side)] * 3,
        mine,
        other,
        gram_one,
        gram_two,
        upper,
        scratch=[pltpu.VMEM((2 * half, side), F32)],
    )


def product(left, right):
    return jnp.dot(left, right, precision=lax.Precision.HIGHEST, preferred_element_type=F32)


def owners():
    pairs = []
    for n in range(256):
        column, j = n // 32, n % 32
        zeta, beyond, core = j // 8, (j % 8) // 2, j % 2
        turn = ((2, 0), (1, 3))[beyond // 2][core]
        x = (column // 2 + turn) % 4
        z = (2 * zeta + beyond % 2 - 2 + 4 * (column % 2)) % 8
        pairs.append((n, (x * 8 + z) * 8 + column))
    return pairs


def at_z(d):
    return lambda b: (jnp.int32(b), lax.rem(lax.axis_index("z") + d + 8, 8))


def at_x(d, first):
    return lambda b: (lax.rem(lax.axis_index("x") + d + 4, 4), jnp.int32(first + b))


def inverted(inverse_pool, panel_one, panel_two, upper_two, lower_one, lower_two, list_one, list_two):
    span, width = panel_one.shape
    both, masked_one, masked_two, keep_one, keep_two = masks(list_one, list_two, panel_one, panel_two)
    moved_two = lax.ppermute(masked_two, ALL, owners())
    moved_one = lax.ppermute(masked_one, ALL, owners())
    tile_hi, tile_lo = split_tile(inverse_pool, span)
    beside = spread(both, "y")
    moved_one, moved_two, tile_hi, tile_lo, beside = lax.optimization_barrier(
        (moved_one, moved_two, tile_hi, tile_lo, beside)
    )

    fans = spread(moved_one, "x")
    ups, downs = [moved_two], [moved_two]
    for s in range(1, 5):
        ups.append(shifted(ups[-1], "z", 1))
        if s < 4:
            downs.append(shifted(downs[-1], "z", -1))
        if s == LEAD:
            fans, ups, downs = lax.optimization_barrier((fans, ups, downs))
    (strip,) = stacked(fans, "x", 1)
    upper, lower = stacked_halves([moved_two, *ups[1:], *downs[:0:-1]], "z")
    sides = []
    for v in (upper, lower):
        for d in (1, -1):
            sides.append(shifted(v, "x", d))
    upper_up, upper_down, lower_up, lower_down = sides
    upper_far = shifted(upper_down, "x", -1)
    lower_far = shifted(lower_up, "x", 1)

    chunks_one = [(strip, 0, at_z(0))]
    up = down = strip
    for s in range(1, 5):
        up = shifted(up, "z", 1)
        chunks_one.append((up, 0, at_z(-s)))
        if s < 4:
            down = shifted(down, "z", -1)
            chunks_one.append((down, 0, at_z(s)))
    chunks_two = [
        (v, 0, at_x(d, first))
        for v, d, first in (
            (upper, 0, 0),
            (lower, 0, 4),
            (upper_up, -1, 0),
            (lower_up, -1, 4),
            (upper_down, 1, 0),
            (lower_down, 1, 4),
            (upper_far, 2, 0),
            (lower_far, 2, 4),
        )
    ]

    keep1, send1 = multiply(tile_hi, tile_lo, chunks_one, width, span)
    came1 = crossed(send1, "k", 1)
    keep2, send2 = multiply(tile_hi, tile_lo, chunks_two, width, span)
    came2 = crossed(send2, "k", 1)
    parts = traded(by_column(keep1, came1, keep2, came2), "y")
    total, keep, send = contract(parts, beside)

    terms = keep + crossed(send, "k", 1)
    terms = jnp.sum(traded(terms.reshape(4, -1, BLK), "x"), axis=0)
    lines = traded(total.reshape(4, span, 2 * BLK), "y")
    for mask in (1, 2, 4):
        terms = terms + crossed(terms, "z", mask)
        if mask == 1:
            terms, gram_one = lax.optimization_barrier((terms, gram(lower_one)))
        if mask == 2:
            terms, lines, gram_two = lax.optimization_barrier((terms, lines, gram(lower_two)))
    mine = traded(jnp.broadcast_to(terms, (16, *terms.shape)), ("x", "y"))
    other = crossed(mine, "k", 1)
    first_diag, second_coupling, second_diag = finish(mine, other, gram_one, gram_two, upper_two)

    product_one = jnp.swapaxes(lines[:, :, :BLK], 0, 1).reshape(span, width)
    product_two = jnp.swapaxes(lines[:, :, BLK:], 0, 1).reshape(span, width)
    first_offdiag = -keep_one[:, :1] * product_one
    second_offdiag = -keep_two[:, :1] * (product(first_offdiag, upper_two) + product_two)
    return (first_offdiag, first_diag, second_offdiag, second_coupling, second_diag)


def solution(mesh):
    finer = Mesh(mesh.devices.reshape(4, 8, 4, 2), ALL)
    rows, columns = ("x", "z"), ("y", "k")
    placed = (P(rows, columns), P(ALL, None), P(ALL, None), P(), P(), P(), P(), P())
    return jax.shard_map(
        inverted,
        mesh=finer,
        in_specs=placed,
        out_specs=(P(ALL, None), P(), P(ALL, None), P(), P()),
        check_vma=False,
    )
```

profile of v0, /device:TPU:1, one launch (start us, length us, event | category | flops | bytes accessed | tf_op | source)
XLA Modules:
  0.0 222.1 jit_solution(187939993407425718)
XLA Ops:
  8.3 9.3 %collective-permute-start = (f32[48,512]{1,0:T(8,128)}, f32[48,512]{1,0:T(8,128)S(1)}, u32[]{:S(2)}, u32[]{:S(2)}) collective-permute-start(f32[48,512]{1,0:T(8,128)} %get-tuple-element.46), channel_id=1, source_target_pairs={{0,176},{1,48},{2,184},{3,56},{4,112},{5,240},{6,120},{7,248},{8,1... | collective-permute-start | bytes 294920 | tf_op jit(solution)/shard_map/ppermute | solution.py:306
  17.6 3.5 %collective-permute-start.1 = (f32[48,512]{1,0:T(8,128)}, f32[48,512]{1,0:T(8,128)S(1)}, u32[]{:S(2)}, u32[]{:S(2)}) collective-permute-start(f32[48,512]{1,0:T(8,128)} %get-tuple-element.47), channel_id=1, source_target_pairs={{0,176},{1,48},{2,184},{3,56},{4,112},{5,240},{6,120},{7,248},{8,1... | collective-permute-start | bytes 294920 | tf_op jit(solution)/shard_map/ppermute | solution.py:305
  21.1 3.4 %shard_map.120 = (bf16[384,1536]{1,0:T(8,128)(2,1)}, bf16[384,1536]{1,0:T(8,128)(2,1)}) custom-call(f32[384,1536]{1,0:T(8,128)} %a.1), custom_call_target="tpu_custom_call" | custom-call | tf_op jit(solution)/shard_map/pallas_call | solution.py:20
  27.4 5.1 %collective-permute-start.5 = (f32[48,512]{1,0:T(8,128)S(1)}, f32[48,512]{1,0:T(8,128)S(1)}, u32[]{:S(2)}, u32[]{:S(2)}) collective-permute-start(f32[48,512]{1,0:T(8,128)S(1)} %collective-permute-done.refs_0_), channel_id=1, source_target_pairs={{0,64},{64,128},{128,192},{192,0},{1,65},{65,129},{129,193},{193,1... | collective-permute-start | bytes 294920 | tf_op jit(solution)/shard_map/ppermute | solution.py:47
  45.5 5.4 %collective-permute-done.12.refs_3_ = f32[192,512]{1,0:T(8,128)S(1)} collective-permute-done((f32[192,512]{1,0:T(8,128)}, f32[192,512]{1,0:T(8,128)S(1)}, u32[]{:S(2)}, u32[]{:S(2)}) %collective-permute-start.12) | collective-permute-done | bytes 393248 | tf_op jit(solution)/shard_map/ppermute | solution.py:47
  50.9 2.7 %collective-permute-start.22 = (f32[48,512]{1,0:T(8,128)S(1)}, f32[48,512]{1,0:T(8,128)S(1)}, u32[]{:S(2)}, u32[]{:S(2)}) collective-permute-start(f32[48,512]{1,0:T(8,128)S(1)} %collective-permute-done.11.refs_6_), channel_id=1, source_target_pairs={{0,56},{8,0},{16,8},{24,16},{32,24},{40,32},{48,40},{56,48},{1,57}... | collective-permute-start | bytes 294920 | tf_op jit(solution)/shard_map/ppermute | solution.py:47
  53.6 7.8 %collective-permute-done.20.refs_3_ = f32[48,512]{1,0:T(8,128)S(1)} collective-permute-done((f32[48,512]{1,0:T(8,128)S(1)}, f32[48,512]{1,0:T(8,128)S(1)}, u32[]{:S(2)}, u32[]{:S(2)}) %collective-permute-start.20) | collective-permute-done | bytes 98336 | tf_op jit(solution)/shard_map/ppermute | solution.py:47
  61.4 6.0 %collective-permute-done.21.refs_4_ = f32[48,512]{1,0:T(8,128)S(1)} collective-permute-done((f32[48,512]{1,0:T(8,128)S(1)}, f32[48,512]{1,0:T(8,128)S(1)}, u32[]{:S(2)}, u32[]{:S(2)}) %collective-permute-start.21) | collective-permute-done | bytes 98336 | tf_op jit(solution)/shard_map/ppermute | solution.py:47
  74.4 2.8 %collective-permute-done.25.refs_6_ = f32[192,512]{1,0:T(8,128)S(1)} collective-permute-done((f32[192,512]{1,0:T(8,128)}, f32[192,512]{1,0:T(8,128)S(1)}, u32[]{:S(2)}, u32[]{:S(2)}) %collective-permute-start.25) | collective-permute-done | bytes 393248 | tf_op jit(solution)/shard_map/ppermute | solution.py:47
  79.2 5.0 %collective-permute-done.23.refs_4_ = f32[192,512]{1,0:T(8,128)S(1)} collective-permute-done((f32[192,512]{1,0:T(8,128)}, f32[192,512]{1,0:T(8,128)S(1)}, u32[]{:S(2)}, u32[]{:S(2)}) %collective-permute-start.23) | collective-permute-done | bytes 393248 | tf_op jit(solution)/shard_map/ppermute | solution.py:47
  87.8 5.0 %collective-permute-done.27.refs_8_ = f32[192,512]{1,0:T(8,128)S(1)} collective-permute-done((f32[192,512]{1,0:T(8,128)S(1)}, f32[192,512]{1,0:T(8,128)S(1)}, u32[]{:S(2)}, u32[]{:S(2)}) %collective-permute-start.27) | collective-permute-done | bytes 393248 | tf_op jit(solution)/shard_map/ppermute | solution.py:47
  96.1 6.0 %shard_map.124 = (f32[192,512]{1,0:T(8,128)}, f32[192,512]{1,0:T(8,128)}) custom-call(bf16[384,1536]{1,0:T(8,128)(2,1)} %get-tuple-element.51.refs_0_, bf16[384,1536]{1,0:T(8,128)(2,1)} %get-tuple-element.52.refs_1_, f32[192,512]{1,0:T(8,128)} %get-tuple-element.65.refs_2_, f32[192,512]{1,0:T(8,128)} %get-tuple-element.66.refs_3_, f32[192,512]{1,0:T(8,128)} %copy-done.13, ...), custom_call_target="tpu_custom_call" | custom-call | tf_op jit(solution)/shard_map/pallas_call | solution.py:20
  102.1 9.5 %collective-permute-start.29 = (f32[192,512]{1,0:T(8,128)}, f32[192,512]{1,0:T(8,128)S(1)}, u32[]{:S(2)}, u32[]{:S(2)}) collective-permute-start(f32[192,512]{1,0:T(8,128)} %get-tuple-element.68), channel_id=1, source_target_pairs={{0,1},{1,0},{2,3},{3,2},{4,5},{5,4},{6,7},{7,6},{8,9},{9,8},{10,11... | collective-permute-start | bytes 1179656 | tf_op jit(solution)/shard_map/ppermute | solution.py:51
  112.4 5.9 %shard_map.122 = (f32[192,512]{1,0:T(8,128)}, f32[192,512]{1,0:T(8,128)}) custom-call(bf16[384,1536]{1,0:T(8,128)(2,1)} %get-tuple-element.51.refs_0_, bf16[384,1536]{1,0:T(8,128)(2,1)} %get-tuple-element.52.refs_1_, f32[192,512]{1,0:T(8,128)} %shard_map.121.refs_2_, f32[192,512]{1,0:T(8,128)} %copy-done.6, f32[192,512]{1,0:T(8,128)} %copy-done.7, ...), custom_call_target="tpu_custom_call" | custom-call | tf_op jit(solution)/shard_map/pallas_call | solution.py:20
  123.4 20.4 %all_to_all.20.ins = f32[4,192,256]{2,1,0:T(8,128)} all-to-all(f32[4,192,256]{2,1,0:T(8,128)} %shard_map.125), channel_id=1, replica_groups=mesh['x'=4,'z'=8,'y'=4,'k'=2] {'y'}, dimensions={0} | all-to-all | bytes 1572864 | tf_op jit(solution)/shard_map/all_to_all | solution.py:55
  143.8 3.4 %shard_map.126 = (f32[192,256]{1,0:T(8,128)}, f32[768,128]{1,0:T(8,128)}, f32[768,128]{1,0:T(8,128)}) custom-call(f32[4,192,256]{2,1,0:T(8,128)} %all_to_all.20.ins, f32[48,1024]{1,0:T(8,128)} %get-tuple-element.69.refs_0_, f32[48,1024]{1,0:T(8,128)} %copy-done.17, f32[48,1024]{1,0:T(8,128)} %copy-done.18, f32[48,1024]{1,0:T(8,128)} %copy-done.19), custom_call_target="tpu_custom_call" | custom-call | tf_op jit(solution)/shard_map/pallas_call | solution.py:20
  150.9 10.2 %all_to_all.21 = f32[4,192,128]{2,1,0:T(8,128)S(1)} all-to-all(f32[4,192,128]{2,1,0:T(8,128)S(1)} %bitcast.16), channel_id=1, replica_groups=mesh['x'=4,'z'=8,'y'=4,'k'=2] {'x'}, dimensions={0} | all-to-all | bytes 786432 | tf_op jit(solution)/shard_map/all_to_all | solution.py:55
  161.2 3.4 %all-to-all-start.2 = ((f32[4,48,256]{2,1,0:T(8,128)}), f32[4,48,256]{2,1,0:T(8,128)S(1)}, u32[]{:S(2)}, u32[]{:S(2)}) async-start(f32[4,48,256]{2,1,0:T(8,128)} %bitcast.3), calls=%async_computation.2 | async-start | bytes 393216 | tf_op jit(solution)/shard_map/all_to_all | solution.py:55
  164.6 3.7 %shard_map.127.g1 = f32[512,512]{1,0:T(8,128)} custom-call(f32[512,512]{1,0:T(8,128)} %ref.2), custom_call_target="tpu_custom_call" | custom-call | tf_op jit(solution)/shard_map/pallas_call | solution.py:20
  168.4 3.7 %shard_map.128.g2 = f32[512,512]{1,0:T(8,128)} custom-call(f32[512,512]{1,0:T(8,128)} %ref.3), custom_call_target="tpu_custom_call" | custom-call | tf_op jit(solution)/shard_map/pallas_call | solution.py:20
  175.1 6.3 %collective-permute-done.33 = f32[192,128]{1,0:T(8,128)S(1)} collective-permute-done((f32[192,128]{1,0:T(8,128)S(1)}, f32[192,128]{1,0:T(8,128)S(1)}, u32[]{:S(2)}, u32[]{:S(2)}) %collective-permute-start.33) | collective-permute-done | bytes 98336 | tf_op jit(solution)/shard_map/ppermute | solution.py:51
  181.6 22.2 %all_to_all.22.own = f32[16,192,128]{2,1,0:T(8,128)S(1)} all-to-all(f32[16,192,128]{2,1,0:T(8,128)S(1)} %broadcast_in_dim.11), channel_id=1, replica_groups=mesh['x'=4,'z'=8,'y'=4,'k'=2] {'x','y'}, dimensions={0} | all-to-all | bytes 3145728 | tf_op jit(solution)/shard_map/all_to_all | solution.py:55
  203.8 6.3 %collective-permute-start.34 = (f32[16,192,128]{2,1,0:T(8,128)S(1)}, f32[16,192,128]{2,1,0:T(8,128)S(1)}, u32[]{:S(2)}, u32[]{:S(2)}) collective-permute-start(f32[16,192,128]{2,1,0:T(8,128)S(1)} %all_to_all.22.own), channel_id=1, source_target_pairs={{0,1},{1,0},{2,3},{3,2},{4,5},{5,4},{6,7},{7,6},{8,9},{9,8},{10,11... | collective-permute-start | bytes 4718600 | tf_op jit(solution)/shard_map/ppermute | solution.py:51
  214.2 7.9 %shard_map.129 = (f32[512,512]{1,0:T(8,128)}, f32[512,512]{1,0:T(8,128)}, f32[512,512]{1,0:T(8,128)}) custom-call(f32[16,192,128]{2,1,0:T(8,128)} %copy-done, f32[16,192,128]{2,1,0:T(8,128)} %copy-done.2, f32[512,512]{1,0:T(8,128)} %shard_map.127.g1, f32[512,512]{1,0:T(8,128)} %shard_map.128.g2, f32[512,512]{1,0:T(8,128)} %u_ref.1), custom_call_target="tpu_custom_call" | custom-call | tf_op jit(solution)/shard_map/pallas_call | solution.py:20
  (140 shorter events, 56.2 us)
Async XLA Ops:
  2.5 22.1 %collective-permute-start.2 = (f32[48,1024]{1,0:T(8,128)}, f32[48,1024]{1,0:T(8,128)S(1)}, u32[]{:S(2)}, u32[]{:S(2)}) collective-permute-start(f32[48,1024]{1,0:T(8,128)} %get-tuple-element.69.refs_0_), channel_id=1, source_target_pairs={{0,2},{2,4},{4,6},{6,0},{1,3},{3,5},{5,7},{7,1},{8,10},{10,12},{12... | collective-permute-start | bytes 589832 | tf_op jit(solution)/shard_map/ppermute | solution.py:47
  4.6 20.0 %collective-permute-start.3 = (f32[48,1024]{1,0:T(8,128)}, f32[48,1024]{1,0:T(8,128)S(1)}, u32[]{:S(2)}, u32[]{:S(2)}) collective-permute-start(f32[48,1024]{1,0:T(8,128)} %get-tuple-element.69.refs_0_), channel_id=1, source_target_pairs={{0,4},{2,6},{4,0},{6,2},{1,5},{3,7},{5,1},{7,3},{8,12},{10,14},{12... | collective-permute-start | bytes 589832 | tf_op jit(solution)/shard_map/ppermute | solution.py:47
  7.2 17.4 %collective-permute-start.4 = (f32[48,1024]{1,0:T(8,128)}, f32[48,1024]{1,0:T(8,128)S(1)}, u32[]{:S(2)}, u32[]{:S(2)}) collective-permute-start(f32[48,1024]{1,0:T(8,128)} %get-tuple-element.69.refs_0_), channel_id=1, source_target_pairs={{0,6},{2,0},{4,2},{6,4},{1,7},{3,1},{5,3},{7,5},{8,14},{10,8},{12,... | collective-permute-start | bytes 589832 | tf_op jit(solution)/shard_map/ppermute | solution.py:47
  8.3 16.3 %collective-permute-start = (f32[48,512]{1,0:T(8,128)}, f32[48,512]{1,0:T(8,128)S(1)}, u32[]{:S(2)}, u32[]{:S(2)}) collective-permute-start(f32[48,512]{1,0:T(8,128)} %get-tuple-element.46), channel_id=1, source_target_pairs={{0,176},{1,48},{2,184},{3,56},{4,112},{5,240},{6,120},{7,248},{8,1... | collective-permute-start | bytes 294920 | tf_op jit(solution)/shard_map/ppermute | solution.py:306
  24.7 10.3 %collective-permute-start.10 = (f32[48,512]{1,0:T(8,128)S(1)}, f32[48,512]{1,0:T(8,128)S(1)}, u32[]{:S(2)}, u32[]{:S(2)}) collective-permute-start(f32[48,512]{1,0:T(8,128)S(1)} %collective-permute-done.1.refs_0_), channel_id=1, source_target_pairs={{0,56},{8,0},{16,8},{24,16},{32,24},{40,32},{48,40},{56,48},{1,57}... | collective-permute-start | bytes 294920 | tf_op jit(solution)/shard_map/ppermute | solution.py:47
  25.8 10.5 %collective-permute-start.8 = (f32[48,512]{1,0:T(8,128)S(1)}, f32[48,512]{1,0:T(8,128)S(1)}, u32[]{:S(2)}, u32[]{:S(2)}) collective-permute-start(f32[48,512]{1,0:T(8,128)S(1)} %collective-permute-done.1.refs_0_), channel_id=1, source_target_pairs={{0,8},{8,16},{16,24},{24,32},{32,40},{40,48},{48,56},{56,0},{1,9},... | collective-permute-start | bytes 294920 | tf_op jit(solution)/shard_map/ppermute | solution.py:47
  27.4 9.0 %collective-permute-start.5 = (f32[48,512]{1,0:T(8,128)S(1)}, f32[48,512]{1,0:T(8,128)S(1)}, u32[]{:S(2)}, u32[]{:S(2)}) collective-permute-start(f32[48,512]{1,0:T(8,128)S(1)} %collective-permute-done.refs_0_), channel_id=1, source_target_pairs={{0,64},{64,128},{128,192},{192,0},{1,65},{65,129},{129,193},{193,1... | collective-permute-start | bytes 294920 | tf_op jit(solution)/shard_map/ppermute | solution.py:47
  42.8 30.1 %collective-permute-start.13 = (f32[192,512]{1,0:T(8,128)}, f32[192,512]{1,0:T(8,128)S(1)}, u32[]{:S(2)}, u32[]{:S(2)}) collective-permute-start(f32[192,512]{1,0:T(8,128)} %shard_map.121.refs_2_), channel_id=1, source_target_pairs={{0,56},{8,0},{16,8},{24,16},{32,24},{40,32},{48,40},{56,48},{1,57}... | collective-permute-start | bytes 1179656 | tf_op jit(solution)/shard_map/ppermute | solution.py:47
  50.9 22.1 %collective-permute-start.14 = (f32[192,512]{1,0:T(8,128)S(1)}, f32[192,512]{1,0:T(8,128)S(1)}, u32[]{:S(2)}, u32[]{:S(2)}) collective-permute-start(f32[192,512]{1,0:T(8,128)S(1)} %collective-permute-done.12.refs_3_), channel_id=1, source_target_pairs={{0,8},{8,16},{16,24},{24,32},{32,40},{40,48},{48,56},{56,0},{1,9},... | collective-permute-start | bytes 1179656 | tf_op jit(solution)/shard_map/ppermute | solution.py:47
  50.9 10.5 %collective-permute-start.20 = (f32[48,512]{1,0:T(8,128)S(1)}, f32[48,512]{1,0:T(8,128)S(1)}, u32[]{:S(2)}, u32[]{:S(2)}) collective-permute-start(f32[48,512]{1,0:T(8,128)S(1)} %collective-permute-done.9.refs_2_), channel_id=1, source_target_pairs={{0,8},{8,16},{16,24},{24,32},{32,40},{40,48},{48,56},{56,0},{1,9},... | collective-permute-start | bytes 294920 | tf_op jit(solution)/shard_map/ppermute | solution.py:47
  50.9 10.5 %collective-permute-start.22 = (f32[48,512]{1,0:T(8,128)S(1)}, f32[48,512]{1,0:T(8,128)S(1)}, u32[]{:S(2)}, u32[]{:S(2)}) collective-permute-start(f32[48,512]{1,0:T(8,128)S(1)} %collective-permute-done.11.refs_6_), channel_id=1, source_target_pairs={{0,56},{8,0},{16,8},{24,16},{32,24},{40,32},{48,40},{56,48},{1,57}... | collective-permute-start | bytes 294920 | tf_op jit(solution)/shard_map/ppermute | solution.py:47
  71.1 8.1 %collective-permute-start.24 = (f32[192,512]{1,0:T(8,128)}, f32[192,512]{1,0:T(8,128)S(1)}, u32[]{:S(2)}, u32[]{:S(2)}) collective-permute-start(f32[192,512]{1,0:T(8,128)} %get-tuple-element.66.refs_3_), channel_id=1, source_target_pairs={{0,64},{64,128},{128,192},{192,0},{1,65},{65,129},{129,193},{193,1... | collective-permute-start | bytes 1179656 | tf_op jit(solution)/shard_map/ppermute | solution.py:47
  71.9 12.3 %collective-permute-start.23 = (f32[192,512]{1,0:T(8,128)}, f32[192,512]{1,0:T(8,128)S(1)}, u32[]{:S(2)}, u32[]{:S(2)}) collective-permute-start(f32[192,512]{1,0:T(8,128)} %get-tuple-element.65.refs_2_), channel_id=1, source_target_pairs={{0,64},{64,128},{128,192},{192,0},{1,65},{65,129},{129,193},{193,1... | collective-permute-start | bytes 1179656 | tf_op jit(solution)/shard_map/ppermute | solution.py:47
  73.0 11.2 %collective-permute-start.15 = (f32[192,512]{1,0:T(8,128)S(1)}, f32[192,512]{1,0:T(8,128)S(1)}, u32[]{:S(2)}, u32[]{:S(2)}) collective-permute-start(f32[192,512]{1,0:T(8,128)S(1)} %collective-permute-done.13.refs_4_), channel_id=1, source_target_pairs={{0,56},{8,0},{16,8},{24,16},{32,24},{40,32},{48,40},{56,48},{1,57}... | collective-permute-start | bytes 1179656 | tf_op jit(solution)/shard_map/ppermute | solution.py:47
  73.0 11.3 %collective-permute-start.16 = (f32[192,512]{1,0:T(8,128)S(1)}, f32[192,512]{1,0:T(8,128)S(1)}, u32[]{:S(2)}, u32[]{:S(2)}) collective-permute-start(f32[192,512]{1,0:T(8,128)S(1)} %collective-permute-done.14.refs_5_), channel_id=1, source_target_pairs={{0,8},{8,16},{16,24},{24,32},{32,40},{40,48},{48,56},{56,0},{1,9},... | collective-permute-start | bytes 1179656 | tf_op jit(solution)/shard_map/ppermute | solution.py:47
  77.2 10.6 %collective-permute-start.26 = (f32[192,512]{1,0:T(8,128)}, f32[192,512]{1,0:T(8,128)S(1)}, u32[]{:S(2)}, u32[]{:S(2)}) collective-permute-start(f32[192,512]{1,0:T(8,128)} %get-tuple-element.66.refs_3_), channel_id=1, source_target_pairs={{0,192},{64,0},{128,64},{192,128},{1,193},{65,1},{129,65},{193,129... | collective-permute-start | bytes 1179656 | tf_op jit(solution)/shard_map/ppermute | solution.py:47
  79.1 13.7 %collective-permute-start.27 = (f32[192,512]{1,0:T(8,128)S(1)}, f32[192,512]{1,0:T(8,128)S(1)}, u32[]{:S(2)}, u32[]{:S(2)}) collective-permute-start(f32[192,512]{1,0:T(8,128)S(1)} %collective-permute-done.25.refs_6_), channel_id=1, source_target_pairs={{0,192},{64,0},{128,64},{192,128},{1,193},{65,1},{129,65},{193,129... | collective-permute-start | bytes 1179656 | tf_op jit(solution)/shard_map/ppermute | solution.py:47
  84.2 11.9 %collective-permute-start.28 = (f32[192,512]{1,0:T(8,128)S(1)}, f32[192,512]{1,0:T(8,128)}, u32[]{:S(2)}, u32[]{:S(2)}) collective-permute-start(f32[192,512]{1,0:T(8,128)S(1)} %collective-permute-done.24.refs_5_), channel_id=1, source_target_pairs={{0,64},{64,128},{128,192},{192,0},{1,65},{65,129},{129,193},{193,1... | collective-permute-start | bytes 1179656 | tf_op jit(solution)/shard_map/ppermute | solution.py:47
  84.2 27.4 %collective-permute-start.17 = (f32[192,512]{1,0:T(8,128)S(1)}, f32[192,512]{1,0:T(8,128)S(1)}, u32[]{:S(2)}, u32[]{:S(2)}) collective-permute-start(f32[192,512]{1,0:T(8,128)S(1)} %collective-permute-done.15.refs_6_), channel_id=1, source_target_pairs={{0,56},{8,0},{16,8},{24,16},{32,24},{40,32},{48,40},{56,48},{1,57}... | collective-permute-start | bytes 1179656 | tf_op jit(solution)/shard_map/ppermute | solution.py:47
  84.3 27.3 %collective-permute-start.18 = (f32[192,512]{1,0:T(8,128)S(1)}, f32[192,512]{1,0:T(8,128)}, u32[]{:S(2)}, u32[]{:S(2)}) collective-permute-start(f32[192,512]{1,0:T(8,128)S(1)} %collective-permute-done.16.refs_7_), channel_id=1, source_target_pairs={{0,8},{8,16},{16,24},{24,32},{32,40},{40,48},{48,56},{56,0},{1,9},... | collective-permute-start | bytes 1179656 | tf_op jit(solution)/shard_map/ppermute | solution.py:47
  102.1 16.2 %collective-permute-start.29 = (f32[192,512]{1,0:T(8,128)}, f32[192,512]{1,0:T(8,128)S(1)}, u32[]{:S(2)}, u32[]{:S(2)}) collective-permute-start(f32[192,512]{1,0:T(8,128)} %get-tuple-element.68), channel_id=1, source_target_pairs={{0,1},{1,0},{2,3},{3,2},{4,5},{5,4},{6,7},{7,6},{8,9},{9,8},{10,11... | collective-permute-start | bytes 1179656 | tf_op jit(solution)/shard_map/ppermute | solution.py:51
  161.2 11.5 %all-to-all-start.2 = ((f32[4,48,256]{2,1,0:T(8,128)}), f32[4,48,256]{2,1,0:T(8,128)S(1)}, u32[]{:S(2)}, u32[]{:S(2)}) async-start(f32[4,48,256]{2,1,0:T(8,128)} %bitcast.3), calls=%async_computation.2 | async-start | bytes 393216 | tf_op jit(solution)/shard_map/all_to_all | solution.py:55
  172.8 8.6 %collective-permute-start.33 = (f32[192,128]{1,0:T(8,128)S(1)}, f32[192,128]{1,0:T(8,128)S(1)}, u32[]{:S(2)}, u32[]{:S(2)}) collective-permute-start(f32[192,128]{1,0:T(8,128)S(1)} %add.17), channel_id=1, source_target_pairs={{0,32},{8,40},{16,48},{24,56},{32,0},{40,8},{48,16},{56,24},{1,33}... | collective-permute-start | bytes 294920 | tf_op jit(solution)/shard_map/ppermute | solution.py:51
  203.8 9.3 %collective-permute-start.34 = (f32[16,192,128]{2,1,0:T(8,128)S(1)}, f32[16,192,128]{2,1,0:T(8,128)S(1)}, u32[]{:S(2)}, u32[]{:S(2)}) collective-permute-start(f32[16,192,128]{2,1,0:T(8,128)S(1)} %all_to_all.22.own), channel_id=1, source_target_pairs={{0,1},{1,0},{2,3},{3,2},{4,5},{5,4},{6,7},{7,6},{8,9},{9,8},{10,11... | collective-permute-start | bytes 4718600 | tf_op jit(solution)/shard_map/ppermute | solution.py:51
  (46 other events, 680.4 us)
where the time goes:
time: 223 us; the launch traced here: 222 us
  starting transfers between devices  66.1 us (30%)
  waiting for transfers between devices  53 us (24%)
  blocking collectives  52.8 us (24%)
  Pallas kernels  42.3 us (19%)
  local copies, waits for them, and re-layouts  4.32 us (2%)
    all_to_all x3, blocking collectives, traded(): return lax.all_to_all(v, axis, split_axis=0, concat_axis=0, tiled=True)  52.8 us
    pallas_call x11, Pallas kernels, call(): pl.pallas_call(body, out_shape=out_shapes, in_specs=[whole] * len(args),...  42.3 us
    ppermute x26, waiting for transfers between devices, shifted(): return lax.ppermute(v, axis, [(i, (i + by) % n) for i in range(n)])  41.1 us
    ppermute x26, starting transfers between devices, shifted(): return lax.ppermute(v, axis, [(i, (i + by) % n) for i in range(n)])  30.5 us
    ppermute x7, starting transfers between devices, crossed(): return lax.ppermute(v, axis, [(i, i ^ mask) for i in range(SIZES[axis])])  19.4 us
    ppermute x7, waiting for transfers between devices, crossed(): return lax.ppermute(v, axis, [(i, i ^ mask) for i in range(SIZES[axis])])  11.9 us
    ppermute x1, starting transfers between devices, inverted(): moved_one = lax.ppermute(masked_one, ALL, owners())  9.32 us
  transfers between devices with their start and end apart: 36, of which 15 were waited for; matrix products, arithmetic and copies ran while one was open for 1% of the time, Pallas kernels for 11%

commit v1 on v0

--- a/solution.py
+++ b/solution.py
@@ -170,45 +170,55 @@
     )
 
 
-def by_column(keep_one, came_one, keep_two, came_two):
-    rows, cols = keep_one.shape
+def by_column(keep, came):
+    rows, cols = keep.shape
     n = cols // BLK
 
-    def body(k1, c1, k2, c2, out):
+    def body(own, far, out):
         for i in range(n):
             at = slice(i * BLK, (i + 1) * BLK)
-            out[i, :, :BLK] = k1[:, at] + c1[:, at]
-            out[i, :, BLK:] = k2[:, at] + c2[:, at]
-
-    return call(body, arr(n, rows, 2 * BLK), keep_one, came_one, keep_two, came_two)
-
-
-def contract(parts, beside):
+            out[i] = own[:, at] + far[:, at]
+
+    return call(body, arr(n, rows, BLK), keep, came)
+
+
+def contract_two(parts, beside):
     n, rows, cols = parts.shape
     span, depth = beside[0].shape
     width = depth // 2
-    half = 3 * width // 2
 
     def body(ins, *refs):
-        total, keep, send, terms, left = refs[n:]
+        total, left, terms = refs[n:]
         for d in range(n):
             left[pl.ds(place("y", -d, span), span), :] = refs[d][...]
         v = ins[0]
         for i in range(1, n):
             v = v + ins[i]
         total[...] = v
-        one = halves(v[:, :BLK])
-        two = halves(v[:, BLK:])
-        terms[: 2 * width, :] = dot3(halves(left[...]), one, ((0,), (0,)))
-        terms[2 * width :, :] = dot3(halves(left[:, width:]), two, ((0,), (0,)))
+        terms[...] = dot3(halves(left[:, width:]), halves(v), ((0,), (0,)))
+
+    return call(body, [arr(rows, cols), arr(rows, depth), arr(width, cols)], parts, *beside)
+
+
+def contract_one(parts, left, total_two, terms_two):
+    n, rows, cols = parts.shape
+    width = terms_two.shape[0]
+    half = 3 * width // 2
+
+    def body(ins, left_ref, other, third, total, keep, send, terms):
+        v = ins[0]
+        for i in range(1, n):
+            v = v + ins[i]
+        total[:, :cols] = v
+        total[:, cols:] = other[...]
+        terms[: 2 * width, :] = dot3(halves(left_ref[...]), halves(v), ((0,), (0,)))
+        terms[2 * width :, :] = third[...]
         k = lax.axis_index("k")
         keep[...] = terms[pl.ds(pl.multiple_of(k * half, half), half), :]
         send[...] = terms[pl.ds(pl.multiple_of((1 - k) * half, half), half), :]
 
-    shapes = [arr(rows, cols)] + [arr(half, BLK)] * 2
-    return call(
-        body, shapes, parts, *beside, scratch=[pltpu.VMEM((2 * half, BLK), F32), pltpu.VMEM((rows, depth), F32)]
-    )
+    shapes = [arr(rows, 2 * cols)] + [arr(half, cols)] * 2
+    return call(body, shapes, parts, left, total_two, terms_two, scratch=[pltpu.VMEM((2 * half, cols), F32)])
 
 
 def in_columns(cols, wide, body):
@@ -305,7 +315,9 @@
     moved_two = lax.ppermute(masked_two, ALL, owners())
     moved_one = lax.ppermute(masked_one, ALL, owners())
     tile_hi, tile_lo = split_tile(inverse_pool, span)
-    beside = spread(both, "y")
+    beside = [both]
+    for d in range(1, 4):
+        beside.append(shifted(both, "y", d))
     moved_one, moved_two, tile_hi, tile_lo, beside = lax.optimization_barrier(
         (moved_one, moved_two, tile_hi, tile_lo, beside)
     )
@@ -327,6 +339,7 @@
     upper_up, upper_down, lower_up, lower_down = sides
     upper_far = shifted(upper_down, "x", -1)
     lower_far = shifted(lower_up, "x", 1)
+    upper_far, gram_one, gram_two = lax.optimization_barrier((upper_far, gram(lower_one), gram(lower_two)))
 
     chunks_one = [(strip, 0, at_z(0))]
     up = down = strip
@@ -350,22 +363,23 @@
         )
     ]
 
+    keep2, send2 = multiply(tile_hi, tile_lo, chunks_two, width, span)
+    parts = traded(by_column(keep2, crossed(send2, "k", 1)), "y")
+    total_two, left, terms_two = contract_two(parts, beside)
+
+    last, terms_two = lax.optimization_barrier((up, terms_two))
+    chunks_one = [(last if v is up else v, c, p) for v, c, p in chunks_one]
     keep1, send1 = multiply(tile_hi, tile_lo, chunks_one, width, span)
-    came1 = crossed(send1, "k", 1)
-    keep2, send2 = multiply(tile_hi, tile_lo, chunks_two, width, span)
-    came2 = crossed(send2, "k", 1)
-    parts = traded(by_column(keep1, came1, keep2, came2), "y")
-    total, keep, send = contract(parts, beside)
+    parts = traded(by_column(keep1, crossed(send1, "k", 1)), "y")
+    total, keep, send = contract_one(parts, left, total_two, terms_two)
 
     terms = keep + crossed(send, "k", 1)
     terms = jnp.sum(traded(terms.reshape(4, -1, BLK), "x"), axis=0)
     lines = traded(total.reshape(4, span, 2 * BLK), "y")
     for mask in (1, 2, 4):
         terms = terms + crossed(terms, "z", mask)
-        if mask == 1:
-            terms, gram_one = lax.optimization_barrier((terms, gram(lower_one)))
         if mask == 2:
-            terms, lines, gram_two = lax.optimization_barrier((terms, lines, gram(lower_two)))
+            terms, lines = lax.optimization_barrier((terms, lines))
     mine = traded(jnp.broadcast_to(terms, (16, *terms.shape)), ("x", "y"))
     other = crossed(mine, "k", 1)
     first_diag, second_coupling, second_diag = finish(mine, other, gram_one, gram_two, upper_two)

time: 223 us -> 217 us (0.973)
  waiting for transfers between devices: 53 us -> 29.7 us
  starting transfers between devices: 66.1 us -> 74.6 us
  Pallas kernels: 42.3 us -> 46.2 us
  blocking collectives: 52.8 us -> 56 us
    ppermute x26, waiting for transfers between devices: 41.1 us -> 20.5 us  [shifted(): return lax.ppermute(v, axis, [(i, (i + by) % n) for i in range(n)])]
    ppermute x7, starting transfers between devices: 19.4 us -> 27.7 us  [crossed(): return lax.ppermute(v, axis, [(i, i ^ mask) for i in range(SIZES[axis])])]
    pallas_call x11 -> x13, Pallas kernels: 42.3 us -> 46.2 us  [call(): pl.pallas_call(body, out_shape=out_shapes, in_specs=[whole] * len(args),...]
    all_to_all x3 -> x4, blocking collectives: 52.8 us -> 56 us  [traded(): return lax.all_to_all(v, axis, split_axis=0, concat_axis=0, tiled=True)]
    ppermute x7, waiting for transfers between devices: 11.9 us -> 8.67 us  [crossed(): return lax.ppermute(v, axis, [(i, i ^ mask) for i in range(SIZES[axis])])]
  transfers between devices with their start and end apart: 36 -> 36, of which waited for: 15 -> 16; matrix products, arithmetic and copies ran while one was open for 1% -> 1% of each run, Pallas kernels for 11% -> 12%
where the time goes in v1:
time: 217 us; the launch traced here: 216 us
  starting transfers between devices  74.6 us (34%)
  blocking collectives  56 us (26%)
  Pallas kernels  46.2 us (21%)
  waiting for transfers between devices  29.7 us (14%)
  local copies, waits for them, and re-layouts  5.53 us (3%)
    all_to_all x4, blocking collectives, traded(): return lax.all_to_all(v, axis, split_axis=0, concat_axis=0, tiled=True)  56 us
    pallas_call x13, Pallas kernels, call(): pl.pallas_call(body, out_shape=out_shapes, in_specs=[whole] * len(args),...  46.2 us
    ppermute x26, starting transfers between devices, shifted(): return lax.ppermute(v, axis, [(i, (i + by) % n) for i in range(n)])  30.7 us
    ppermute x7, starting transfers between devices, crossed(): return lax.ppermute(v, axis, [(i, i ^ mask) for i in range(SIZES[axis])])  27.7 us
    ppermute x26, waiting for transfers between devices, shifted(): return lax.ppermute(v, axis, [(i, (i + by) % n) for i in range(n)])  20.5 us
    ppermute x1, starting transfers between devices, inverted(): moved_one = lax.ppermute(masked_one, ALL, owners())  9.32 us
    ppermute x7, waiting for transfers between devices, crossed(): return lax.ppermute(v, axis, [(i, i ^ mask) for i in range(SIZES[axis])])  8.67 us
    unnamed x69, local copies, waits for them, and re-layouts  5.38 us
  transfers between devices with their start and end apart: 36, of which 16 were waited for; matrix products, arithmetic and copies ran while one was open for 1% of the time, Pallas kernels for 12%

profile of v1, /device:TPU:1, one launch (start us, length us, event | category | flops | bytes accessed | tf_op | source)
XLA Modules:
  0.0 215.7 jit_solution(14252670833149406580)
XLA Ops:
  2.5 3.6 %collective-permute-start.4 = (f32[48,1024]{1,0:T(8,128)}, f32[48,1024]{1,0:T(8,128)S(1)}, u32[]{:S(2)}, u32[]{:S(2)}) collective-permute-start(f32[48,1024]{1,0:T(8,128)} %get-tuple-element.73.refs_0_), channel_id=1, source_target_pairs={{0,6},{2,0},{4,2},{6,4},{1,7},{3,1},{5,3},{7,5},{8,14},{10,8},{12,... | collective-permute-start | bytes 589832 | tf_op jit(solution)/shard_map/ppermute | solution.py:47
  7.1 9.3 %collective-permute-start = (f32[48,512]{1,0:T(8,128)}, f32[48,512]{1,0:T(8,128)S(1)}, u32[]{:S(2)}, u32[]{:S(2)}) collective-permute-start(f32[48,512]{1,0:T(8,128)} %get-tuple-element.51), channel_id=1, source_target_pairs={{0,176},{1,48},{2,184},{3,56},{4,112},{5,240},{6,120},{7,248},{8,1... | collective-permute-start | bytes 294920 | tf_op jit(solution)/shard_map/ppermute | solution.py:316
  16.4 3.5 %collective-permute-start.1 = (f32[48,512]{1,0:T(8,128)}, f32[48,512]{1,0:T(8,128)S(1)}, u32[]{:S(2)}, u32[]{:S(2)}) collective-permute-start(f32[48,512]{1,0:T(8,128)} %get-tuple-element.52), channel_id=1, source_target_pairs={{0,176},{1,48},{2,184},{3,56},{4,112},{5,240},{6,120},{7,248},{8,1... | collective-permute-start | bytes 294920 | tf_op jit(solution)/shard_map/ppermute | solution.py:315
  19.9 3.4 %shard_map.120 = (bf16[384,1536]{1,0:T(8,128)(2,1)}, bf16[384,1536]{1,0:T(8,128)(2,1)}) custom-call(f32[384,1536]{1,0:T(8,128)} %a.1), custom_call_target="tpu_custom_call" | custom-call | tf_op jit(solution)/shard_map/pallas_call | solution.py:20
  26.2 7.8 %collective-permute-start.7 = (f32[48,512]{1,0:T(8,128)S(1)}, f32[48,512]{1,0:T(8,128)S(1)}, u32[]{:S(2)}, u32[]{:S(2)}) collective-permute-start(f32[48,512]{1,0:T(8,128)S(1)} %collective-permute-done.refs_0_), channel_id=1, source_target_pairs={{0,192},{64,0},{128,64},{192,128},{1,193},{65,1},{129,65},{193,129... | collective-permute-start | bytes 294920 | tf_op jit(solution)/shard_map/ppermute | solution.py:47
  47.4 2.8 %collective-permute-done.20.refs_4_ = f32[48,512]{1,0:T(8,128)S(1)} collective-permute-done((f32[48,512]{1,0:T(8,128)S(1)}, f32[48,512]{1,0:T(8,128)S(1)}, u32[]{:S(2)}, u32[]{:S(2)}) %collective-permute-start.20) | collective-permute-done | bytes 98336 | tf_op jit(solution)/shard_map/ppermute | solution.py:47
  57.3 3.7 %collective-permute-done.24.refs_6_ = f32[192,512]{1,0:T(8,128)S(1)} collective-permute-done((f32[192,512]{1,0:T(8,128)}, f32[192,512]{1,0:T(8,128)S(1)}, u32[]{:S(2)}, u32[]{:S(2)}) %collective-permute-start.24) | collective-permute-done | bytes 393248 | tf_op jit(solution)/shard_map/ppermute | solution.py:47
  61.0 2.7 %collective-permute-start.26 = (f32[192,512]{1,0:T(8,128)S(1)}, f32[192,512]{1,0:T(8,128)S(1)}, u32[]{:S(2)}, u32[]{:S(2)}) collective-permute-start(f32[192,512]{1,0:T(8,128)S(1)} %collective-permute-done.24.refs_6_), channel_id=1, source_target_pairs={{0,192},{64,0},{128,64},{192,128},{1,193},{65,1},{129,65},{193,129... | collective-permute-start | bytes 1179656 | tf_op jit(solution)/shard_map/ppermute | solution.py:47
  66.5 5.5 %collective-permute-done.26.refs_8_ = f32[192,512]{1,0:T(8,128)S(1)} collective-permute-done((f32[192,512]{1,0:T(8,128)S(1)}, f32[192,512]{1,0:T(8,128)S(1)}, u32[]{:S(2)}, u32[]{:S(2)}) %collective-permute-start.26) | collective-permute-done | bytes 393248 | tf_op jit(solution)/shard_map/ppermute | solution.py:47
  72.0 3.8 %shard_map.123.g1 = f32[512,512]{1,0:T(8,128)} custom-call(f32[512,512]{1,0:T(8,128)} %ref.2), custom_call_target="tpu_custom_call" | custom-call | tf_op jit(solution)/shard_map/pallas_call | solution.py:20
  75.8 3.7 %shard_map.124.g2 = f32[512,512]{1,0:T(8,128)} custom-call(f32[512,512]{1,0:T(8,128)} %ref.3), custom_call_target="tpu_custom_call" | custom-call | tf_op jit(solution)/shard_map/pallas_call | solution.py:20
  80.3 6.0 %shard_map.125 = (f32[192,512]{1,0:T(8,128)}, f32[192,512]{1,0:T(8,128)}) custom-call(bf16[384,1536]{1,0:T(8,128)(2,1)} %get-tuple-element.56.refs_0_, bf16[384,1536]{1,0:T(8,128)(2,1)} %get-tuple-element.57.refs_1_, f32[192,512]{1,0:T(8,128)} %get-tuple-element.68.refs_2_, f32[192,512]{1,0:T(8,128)} %get-tuple-element.69.refs_3_, f32[192,512]{1,0:T(8,128)} %copy-done.14, ...), custom_call_target="tpu_custom_call" | custom-call | tf_op jit(solution)/shard_map/pallas_call | solution.py:20
  86.3 9.0 %collective-permute-start.28 = (f32[192,512]{1,0:T(8,128)}, f32[192,512]{1,0:T(8,128)S(1)}, u32[]{:S(2)}, u32[]{:S(2)}) collective-permute-start(f32[192,512]{1,0:T(8,128)} %get-tuple-element.72), channel_id=1, source_target_pairs={{0,1},{1,0},{2,3},{3,2},{4,5},{5,4},{6,7},{7,6},{8,9},{9,8},{10,11... | collective-permute-start | bytes 1179656 | tf_op jit(solution)/shard_map/ppermute | solution.py:51
  100.7 11.9 %all_to_all.25.ins = f32[4,192,128]{2,1,0:T(8,128)} all-to-all(f32[4,192,128]{2,1,0:T(8,128)} %shard_map.126), channel_id=1, replica_groups=mesh['x'=4,'z'=8,'y'=4,'k'=2] {'y'}, dimensions={0} | all-to-all | bytes 786432 | tf_op jit(solution)/shard_map/all_to_all | solution.py:55
  112.6 2.7 %shard_map.127 = (f32[192,128]{1,0:T(8,128)}, f32[192,1024]{1,0:T(8,128)}, f32[512,128]{1,0:T(8,128)}) custom-call(f32[4,192,128]{2,1,0:T(8,128)} %all_to_all.25.ins, f32[48,1024]{1,0:T(8,128)} %get-tuple-element.73.refs_0_, f32[48,1024]{1,0:T(8,128)} %copy-done.19, f32[48,1024]{1,0:T(8,128)} %copy-done.18, f32[48,1024]{1,0:T(8,128)} %copy-done.17), custom_call_target="tpu_custom_call" | custom-call | tf_op jit(solution)/shard_map/pallas_call | solution.py:20
  116.8 6.0 %shard_map.128 = (f32[192,512]{1,0:T(8,128)}, f32[192,512]{1,0:T(8,128)}) custom-call(bf16[384,1536]{1,0:T(8,128)(2,1)} %get-tuple-element.56.refs_0_, bf16[384,1536]{1,0:T(8,128)(2,1)} %get-tuple-element.57.refs_1_, f32[192,512]{1,0:T(8,128)} %shard_map.121.refs_2_, f32[192,512]{1,0:T(8,128)} %copy-done.6, f32[192,512]{1,0:T(8,128)} %copy-done.7, ...), custom_call_target="tpu_custom_call" | custom-call | tf_op jit(solution)/shard_map/pallas_call | solution.py:20
  128.7 12.0 %all_to_all.26.ins = f32[4,192,128]{2,1,0:T(8,128)} all-to-all(f32[4,192,128]{2,1,0:T(8,128)} %shard_map.129), channel_id=1, replica_groups=mesh['x'=4,'z'=8,'y'=4,'k'=2] {'y'}, dimensions={0} | all-to-all | bytes 786432 | tf_op jit(solution)/shard_map/all_to_all | solution.py:55
  140.7 3.0 %shard_map.130 = (f32[192,256]{1,0:T(8,128)}, f32[768,128]{1,0:T(8,128)}, f32[768,128]{1,0:T(8,128)}) custom-call(f32[4,192,128]{2,1,0:T(8,128)} %all_to_all.26.ins, f32[192,1024]{1,0:T(8,128)} %get-tuple-element.81.left_ref, f32[192,128]{1,0:T(8,128)} %get-tuple-element.82.other, f32[512,128]{1,0:T(8,128)} %get-tuple-element.83.third), custom_call_target="tpu_custom_call" | custom-call | tf_op jit(solution)/shard_map/pallas_call | solution.py:20
  147.5 11.2 %all_to_all.27 = f32[4,192,128]{2,1,0:T(8,128)S(1)} all-to-all(f32[4,192,128]{2,1,0:T(8,128)S(1)} %bitcast.16), channel_id=1, replica_groups=mesh['x'=4,'z'=8,'y'=4,'k'=2] {'x'}, dimensions={0} | all-to-all | bytes 786432 | tf_op jit(solution)/shard_map/all_to_all | solution.py:55
  158.9 3.4 %all-to-all-start.3 = ((f32[4,48,256]{2,1,0:T(8,128)}), f32[4,48,256]{2,1,0:T(8,128)S(1)}, u32[]{:S(2)}, u32[]{:S(2)}) async-start(f32[4,48,256]{2,1,0:T(8,128)} %bitcast.3), calls=%async_computation.3 | async-start | bytes 393216 | tf_op jit(solution)/shard_map/all_to_all | solution.py:55
  167.4 5.4 %collective-permute-start.33 = (f32[192,128]{1,0:T(8,128)S(1)}, f32[192,128]{1,0:T(8,128)S(1)}, u32[]{:S(2)}, u32[]{:S(2)}) collective-permute-start(f32[192,128]{1,0:T(8,128)S(1)} %add.17), channel_id=1, source_target_pairs={{0,32},{8,40},{16,48},{24,56},{32,0},{40,8},{48,16},{56,24},{1,33}... | collective-permute-start | bytes 294920 | tf_op jit(solution)/shard_map/ppermute | solution.py:51
  175.1 21.0 %all_to_all.28.own = f32[16,192,128]{2,1,0:T(8,128)S(1)} all-to-all(f32[16,192,128]{2,1,0:T(8,128)S(1)} %broadcast_in_dim.11), channel_id=1, replica_groups=mesh['x'=4,'z'=8,'y'=4,'k'=2] {'x','y'}, dimensions={0} | all-to-all | bytes 3145728 | tf_op jit(solution)/shard_map/all_to_all | solution.py:55
  196.1 7.6 %collective-permute-start.34 = (f32[16,192,128]{2,1,0:T(8,128)S(1)}, f32[16,192,128]{2,1,0:T(8,128)S(1)}, u32[]{:S(2)}, u32[]{:S(2)}) collective-permute-start(f32[16,192,128]{2,1,0:T(8,128)S(1)} %all_to_all.28.own), channel_id=1, source_target_pairs={{0,1},{1,0},{2,3},{3,2},{4,5},{5,4},{6,7},{7,6},{8,9},{9,8},{10,11... | collective-permute-start | bytes 4718600 | tf_op jit(solution)/shard_map/ppermute | solution.py:51
  207.8 7.9 %shard_map.131 = (f32[512,512]{1,0:T(8,128)}, f32[512,512]{1,0:T(8,128)}, f32[512,512]{1,0:T(8,128)}) custom-call(f32[16,192,128]{2,1,0:T(8,128)} %copy-done, f32[16,192,128]{2,1,0:T(8,128)} %copy-done.2, f32[512,512]{1,0:T(8,128)} %shard_map.123.g1, f32[512,512]{1,0:T(8,128)} %shard_map.124.g2, f32[512,512]{1,0:T(8,128)} %u_ref.1), custom_call_target="tpu_custom_call" | custom-call | tf_op jit(solution)/shard_map/pallas_call | solution.py:20
  (143 shorter events, 57.9 us)
Async XLA Ops:
  2.5 20.9 %collective-permute-start.4 = (f32[48,1024]{1,0:T(8,128)}, f32[48,1024]{1,0:T(8,128)S(1)}, u32[]{:S(2)}, u32[]{:S(2)}) collective-permute-start(f32[48,1024]{1,0:T(8,128)} %get-tuple-element.73.refs_0_), channel_id=1, source_target_pairs={{0,6},{2,0},{4,2},{6,4},{1,7},{3,1},{5,3},{7,5},{8,14},{10,8},{12,... | collective-permute-start | bytes 589832 | tf_op jit(solution)/shard_map/ppermute | solution.py:47
  6.0 17.4 %collective-permute-start.3 = (f32[48,1024]{1,0:T(8,128)}, f32[48,1024]{1,0:T(8,128)S(1)}, u32[]{:S(2)}, u32[]{:S(2)}) collective-permute-start(f32[48,1024]{1,0:T(8,128)} %get-tuple-element.73.refs_0_), channel_id=1, source_target_pairs={{0,4},{2,6},{4,0},{6,2},{1,5},{3,7},{5,1},{7,3},{8,12},{10,14},{12... | collective-permute-start | bytes 589832 | tf_op jit(solution)/shard_map/ppermute | solution.py:47
  6.4 17.1 %collective-permute-start.2 = (f32[48,1024]{1,0:T(8,128)}, f32[48,1024]{1,0:T(8,128)S(1)}, u32[]{:S(2)}, u32[]{:S(2)}) collective-permute-start(f32[48,1024]{1,0:T(8,128)} %get-tuple-element.73.refs_0_), channel_id=1, source_target_pairs={{0,2},{2,4},{4,6},{6,0},{1,3},{3,5},{5,7},{7,1},{8,10},{10,12},{12... | collective-permute-start | bytes 589832 | tf_op jit(solution)/shard_map/ppermute | solution.py:47
  7.1 16.3 %collective-permute-start = (f32[48,512]{1,0:T(8,128)}, f32[48,512]{1,0:T(8,128)S(1)}, u32[]{:S(2)}, u32[]{:S(2)}) collective-permute-start(f32[48,512]{1,0:T(8,128)} %get-tuple-element.51), channel_id=1, source_target_pairs={{0,176},{1,48},{2,184},{3,56},{4,112},{5,240},{6,120},{7,248},{8,1... | collective-permute-start | bytes 294920 | tf_op jit(solution)/shard_map/ppermute | solution.py:316
  23.4 11.1 %collective-permute-start.10 = (f32[48,512]{1,0:T(8,128)S(1)}, f32[48,512]{1,0:T(8,128)S(1)}, u32[]{:S(2)}, u32[]{:S(2)}) collective-permute-start(f32[48,512]{1,0:T(8,128)S(1)} %collective-permute-done.1.refs_0_), channel_id=1, source_target_pairs={{0,56},{8,0},{16,8},{24,16},{32,24},{40,32},{48,40},{56,48},{1,57}... | collective-permute-start | bytes 294920 | tf_op jit(solution)/shard_map/ppermute | solution.py:47
  24.6 11.3 %collective-permute-start.8 = (f32[48,512]{1,0:T(8,128)S(1)}, f32[48,512]{1,0:T(8,128)S(1)}, u32[]{:S(2)}, u32[]{:S(2)}) collective-permute-start(f32[48,512]{1,0:T(8,128)S(1)} %collective-permute-done.1.refs_0_), channel_id=1, source_target_pairs={{0,8},{8,16},{16,24},{24,32},{32,40},{40,48},{48,56},{56,0},{1,9},... | collective-permute-start | bytes 294920 | tf_op jit(solution)/shard_map/ppermute | solution.py:47
  26.2 10.4 %collective-permute-start.7 = (f32[48,512]{1,0:T(8,128)S(1)}, f32[48,512]{1,0:T(8,128)S(1)}, u32[]{:S(2)}, u32[]{:S(2)}) collective-permute-start(f32[48,512]{1,0:T(8,128)S(1)} %collective-permute-done.refs_0_), channel_id=1, source_target_pairs={{0,192},{64,0},{128,64},{192,128},{1,193},{65,1},{129,65},{193,129... | collective-permute-start | bytes 294920 | tf_op jit(solution)/shard_map/ppermute | solution.py:47
  47.4 9.9 %collective-permute-start.12 = (f32[192,512]{1,0:T(8,128)}, f32[192,512]{1,0:T(8,128)S(1)}, u32[]{:S(2)}, u32[]{:S(2)}) collective-permute-start(f32[192,512]{1,0:T(8,128)} %shard_map.121.refs_2_), channel_id=1, source_target_pairs={{0,8},{8,16},{16,24},{24,32},{32,40},{40,48},{48,56},{56,0},{1,9},... | collective-permute-start | bytes 1179656 | tf_op jit(solution)/shard_map/ppermute | solution.py:47
  53.1 7.9 %collective-permute-start.24 = (f32[192,512]{1,0:T(8,128)}, f32[192,512]{1,0:T(8,128)S(1)}, u32[]{:S(2)}, u32[]{:S(2)}) collective-permute-start(f32[192,512]{1,0:T(8,128)} %get-tuple-element.68.refs_2_), channel_id=1, source_target_pairs={{0,192},{64,0},{128,64},{192,128},{1,193},{65,1},{129,65},{193,129... | collective-permute-start | bytes 1179656 | tf_op jit(solution)/shard_map/ppermute | solution.py:47
  55.3 8.4 %collective-permute-start.13 = (f32[192,512]{1,0:T(8,128)}, f32[192,512]{1,0:T(8,128)S(1)}, u32[]{:S(2)}, u32[]{:S(2)}) collective-permute-start(f32[192,512]{1,0:T(8,128)} %shard_map.121.refs_2_), channel_id=1, source_target_pairs={{0,56},{8,0},{16,8},{24,16},{32,24},{40,32},{48,40},{56,48},{1,57}... | collective-permute-start | bytes 1179656 | tf_op jit(solution)/shard_map/ppermute | solution.py:47
  55.4 11.0 %collective-permute-start.23 = (f32[192,512]{1,0:T(8,128)}, f32[192,512]{1,0:T(8,128)S(1)}, u32[]{:S(2)}, u32[]{:S(2)}) collective-permute-start(f32[192,512]{1,0:T(8,128)} %get-tuple-element.69.refs_3_), channel_id=1, source_target_pairs={{0,64},{64,128},{128,192},{192,0},{1,65},{65,129},{129,193},{193,1... | collective-permute-start | bytes 1179656 | tf_op jit(solution)/shard_map/ppermute | solution.py:47
  57.3 9.1 %collective-permute-start.14 = (f32[192,512]{1,0:T(8,128)S(1)}, f32[192,512]{1,0:T(8,128)S(1)}, u32[]{:S(2)}, u32[]{:S(2)}) collective-permute-start(f32[192,512]{1,0:T(8,128)S(1)} %collective-permute-done.12.refs_3_), channel_id=1, source_target_pairs={{0,8},{8,16},{16,24},{24,32},{32,40},{40,48},{48,56},{56,0},{1,9},... | collective-permute-start | bytes 1179656 | tf_op jit(solution)/shard_map/ppermute | solution.py:47
  61.0 11.0 %collective-permute-start.26 = (f32[192,512]{1,0:T(8,128)S(1)}, f32[192,512]{1,0:T(8,128)S(1)}, u32[]{:S(2)}, u32[]{:S(2)}) collective-permute-start(f32[192,512]{1,0:T(8,128)S(1)} %collective-permute-done.24.refs_6_), channel_id=1, source_target_pairs={{0,192},{64,0},{128,64},{192,128},{1,193},{65,1},{129,65},{193,129... | collective-permute-start | bytes 1179656 | tf_op jit(solution)/shard_map/ppermute | solution.py:47
  63.7 15.8 %collective-permute-start.22 = (f32[192,512]{1,0:T(8,128)}, f32[192,512]{1,0:T(8,128)S(1)}, u32[]{:S(2)}, u32[]{:S(2)}) collective-permute-start(f32[192,512]{1,0:T(8,128)} %get-tuple-element.68.refs_2_), channel_id=1, source_target_pairs={{0,64},{64,128},{128,192},{192,0},{1,65},{65,129},{129,193},{193,1... | collective-permute-start | bytes 1179656 | tf_op jit(solution)/shard_map/ppermute | solution.py:47
  63.7 15.8 %collective-permute-start.25 = (f32[192,512]{1,0:T(8,128)}, f32[192,512]{1,0:T(8,128)}, u32[]{:S(2)}, u32[]{:S(2)}) collective-permute-start(f32[192,512]{1,0:T(8,128)} %get-tuple-element.69.refs_3_), channel_id=1, source_target_pairs={{0,192},{64,0},{128,64},{192,128},{1,193},{65,1},{129,65},{193,129... | collective-permute-start | bytes 1179656 | tf_op jit(solution)/shard_map/ppermute | solution.py:47
  66.4 13.4 %collective-permute-start.27 = (f32[192,512]{1,0:T(8,128)S(1)}, f32[192,512]{1,0:T(8,128)}, u32[]{:S(2)}, u32[]{:S(2)}) collective-permute-start(f32[192,512]{1,0:T(8,128)S(1)} %collective-permute-done.23.refs_5_), channel_id=1, source_target_pairs={{0,64},{64,128},{128,192},{192,0},{1,65},{65,129},{129,193},{193,1... | collective-permute-start | bytes 1179656 | tf_op jit(solution)/shard_map/ppermute | solution.py:47
  66.4 28.9 %collective-permute-start.16 = (f32[192,512]{1,0:T(8,128)S(1)}, f32[192,512]{1,0:T(8,128)S(1)}, u32[]{:S(2)}, u32[]{:S(2)}) collective-permute-start(f32[192,512]{1,0:T(8,128)S(1)} %collective-permute-done.14.refs_5_), channel_id=1, source_target_pairs={{0,8},{8,16},{16,24},{24,32},{32,40},{40,48},{48,56},{56,0},{1,9},... | collective-permute-start | bytes 1179656 | tf_op jit(solution)/shard_map/ppermute | solution.py:47
  72.0 24.7 %collective-permute-start.15 = (f32[192,512]{1,0:T(8,128)S(1)}, f32[192,512]{1,0:T(8,128)S(1)}, u32[]{:S(2)}, u32[]{:S(2)}) collective-permute-start(f32[192,512]{1,0:T(8,128)S(1)} %collective-permute-done.13.refs_4_), channel_id=1, source_target_pairs={{0,56},{8,0},{16,8},{24,16},{32,24},{40,32},{48,40},{56,48},{1,57}... | collective-permute-start | bytes 1179656 | tf_op jit(solution)/shard_map/ppermute | solution.py:47
  86.3 11.7 %collective-permute-start.28 = (f32[192,512]{1,0:T(8,128)}, f32[192,512]{1,0:T(8,128)S(1)}, u32[]{:S(2)}, u32[]{:S(2)}) collective-permute-start(f32[192,512]{1,0:T(8,128)} %get-tuple-element.72), channel_id=1, source_target_pairs={{0,1},{1,0},{2,3},{3,2},{4,5},{5,4},{6,7},{7,6},{8,9},{9,8},{10,11... | collective-permute-start | bytes 1179656 | tf_op jit(solution)/shard_map/ppermute | solution.py:51
  95.3 19.9 %collective-permute-start.18 = (f32[192,512]{1,0:T(8,128)S(1)}, f32[192,512]{1,0:T(8,128)S(1)}, u32[]{:S(2)}, u32[]{:S(2)}) collective-permute-start(f32[192,512]{1,0:T(8,128)S(1)} %collective-permute-done.16.refs_7_), channel_id=1, source_target_pairs={{0,8},{8,16},{16,24},{24,32},{32,40},{40,48},{48,56},{56,0},{1,9},... | collective-permute-start | bytes 1179656 | tf_op jit(solution)/shard_map/ppermute | solution.py:47
  96.7 18.5 %collective-permute-start.17 = (f32[192,512]{1,0:T(8,128)S(1)}, f32[192,512]{1,0:T(8,128)S(1)}, u32[]{:S(2)}, u32[]{:S(2)}) collective-permute-start(f32[192,512]{1,0:T(8,128)S(1)} %collective-permute-done.15.refs_6_), channel_id=1, source_target_pairs={{0,56},{8,0},{16,8},{24,16},{32,24},{40,32},{48,40},{56,48},{1,57}... | collective-permute-start | bytes 1179656 | tf_op jit(solution)/shard_map/ppermute | solution.py:47
  158.9 8.5 %all-to-all-start.3 = ((f32[4,48,256]{2,1,0:T(8,128)}), f32[4,48,256]{2,1,0:T(8,128)S(1)}, u32[]{:S(2)}, u32[]{:S(2)}) async-start(f32[4,48,256]{2,1,0:T(8,128)} %bitcast.3), calls=%async_computation.3 | async-start | bytes 393216 | tf_op jit(solution)/shard_map/all_to_all | solution.py:55
  167.4 7.5 %collective-permute-start.33 = (f32[192,128]{1,0:T(8,128)S(1)}, f32[192,128]{1,0:T(8,128)S(1)}, u32[]{:S(2)}, u32[]{:S(2)}) collective-permute-start(f32[192,128]{1,0:T(8,128)S(1)} %add.17), channel_id=1, source_target_pairs={{0,32},{8,40},{16,48},{24,56},{32,0},{40,8},{48,16},{56,24},{1,33}... | collective-permute-start | bytes 294920 | tf_op jit(solution)/shard_map/ppermute | solution.py:51
  196.1 10.6 %collective-permute-start.34 = (f32[16,192,128]{2,1,0:T(8,128)S(1)}, f32[16,192,128]{2,1,0:T(8,128)S(1)}, u32[]{:S(2)}, u32[]{:S(2)}) collective-permute-start(f32[16,192,128]{2,1,0:T(8,128)S(1)} %all_to_all.28.own), channel_id=1, source_target_pairs={{0,1},{1,0},{2,3},{3,2},{4,5},{5,4},{6,7},{7,6},{8,9},{9,8},{10,11... | collective-permute-start | bytes 4718600 | tf_op jit(solution)/shard_map/ppermute | solution.py:51
  (46 other events, 510.0 us)

commit v2 on v0

--- a/solution.py
+++ b/solution.py
@@ -64,24 +64,40 @@
     return pl.multiple_of(lax.rem(lax.axis_index(axis) + (n + d) % n, n) * step, step)
 
 
+def live_at(listing, first, rows):
+    row = lax.broadcasted_iota(jnp.int32, (rows, listing.shape[1]), 0) + first
+    hits = jnp.where(lax.shift_right_logical(row, 7) == listing[...], 1.0, 0.0).astype(F32)
+    return jnp.max(hits, axis=1, keepdims=True)
+
+
 def masks(list_one, list_two, panel_one, panel_two):
     rows, cols = panel_one.shape
 
-    def body(one_list, two_list, one, two, both, out1, out2, keep1, keep2):
+    def body(one_list, two_list, one, two, both, keep1, keep2):
         index = lax.axis_index("x")
         for axis in ("z", "y", "k"):
             index = index * SIZES[axis] + lax.axis_index(axis)
-        for listing, panel, out, keep, at in ((one_list, one, out1, keep1, 0), (two_list, two, out2, keep2, cols)):
-            row = lax.broadcasted_iota(jnp.int32, (rows, listing.shape[1]), 0) + index * rows
-            hits = jnp.where(lax.shift_right_logical(row, 7) == listing[...], 1.0, 0.0).astype(F32)
-            live = jnp.max(hits, axis=1, keepdims=True)
+        for listing, panel, keep, at in ((one_list, one, keep1, 0), (two_list, two, keep2, cols)):
+            live = live_at(listing, index * rows, rows)
             keep[...] = jnp.broadcast_to(live, (rows, BLK))
-            v = live * panel[...]
-            out[...] = v
-            both[:, at : at + cols] = v
-
-    shapes = [arr(rows, 2 * cols)] + [arr(rows, cols)] * 2 + [arr(rows, BLK)] * 2
+            both[:, at : at + cols] = live * panel[...]
+
+    shapes = [arr(rows, 2 * cols), arr(rows, BLK), arr(rows, BLK)]
     return call(body, shapes, list_one[None], list_two[None], panel_one, panel_two)
+
+
+def column_masks(list_one, list_two, depth):
+    def body(one_list, two_list, live1, live2):
+        first = (lax.axis_index("y") * 2 + lax.axis_index("k")) * depth
+        for listing, out in ((one_list, live1), (two_list, live2)):
+            def put(i, carry, listing=listing, out=out):
+                at = pl.multiple_of(i * BLK, BLK)
+                out[pl.ds(at, BLK), :] = jnp.broadcast_to(live_at(listing, first + at, BLK), (BLK, BLK))
+                return carry
+
+            lax.fori_loop(0, depth // BLK, put, 0)
+
+    return call(body, [arr(depth, BLK)] * 2, list_one[None], list_two[None])
 
 
 def split_tile(tile, span):
@@ -136,20 +152,26 @@
     return lax.shift_right_logical(order, 1) * 8 + lax.rem(order, 2) * 2 + side
 
 
-def multiply(tile_hi, tile_lo, chunks, cols, span):
+def multiply(tile_hi, tile_lo, live, chunks, cols, span):
     rows, depth = tile_hi.shape
     m = len(chunks)
     wide = 256
 
     def body(*refs):
-        hi, lo = refs[0], refs[1]
-        keep, send, b_hi, b_lo = refs[2 + m :]
-        for ref, (_, column, at_of) in zip(refs[2 : 2 + m], chunks):
-            for b in range(ref.shape[0] // span):
-                h, l = halves(ref[b * span : (b + 1) * span, :])
+        hi, lo, kept = refs[:3]
+        keep, send, b_hi, b_lo = refs[3 + m :]
+        for ref, (_, at_of) in zip(refs[3 : 3 + m], chunks):
+            def put(b, carry, ref=ref, at_of=at_of):
                 at = pl.ds(pl.multiple_of(spot(*at_of(b)) * span, span), span)
-                b_hi[at, column : column + ref.shape[1]] = h
-                b_lo[at, column : column + ref.shape[1]] = l
+                rows_at = pl.ds(pl.multiple_of(b * span, span), span)
+                mask = kept[at, :]
+                for c in range(0, cols, BLK):
+                    h, l = halves(mask * ref[rows_at, c : c + BLK])
+                    b_hi[at, c : c + BLK] = h
+                    b_lo[at, c : c + BLK] = l
+                return carry
+
+            lax.fori_loop(0, ref.shape[0] // span, put, 0)
 
         def step(i, carry):
             at = pl.ds(pl.multiple_of(i * wide, wide), wide)
@@ -165,37 +187,59 @@
         [arr(rows // 2, cols)] * 2,
         tile_hi,
         tile_lo,
+        live,
         *[c[0] for c in chunks],
         scratch=[pltpu.VMEM((depth, cols), BF16)] * 2,
     )
 
 
 def by_column(keep_one, came_one, keep_two, came_two):
-    rows, cols = keep_one.shape
-    n = cols // BLK
-
-    def body(k1, c1, k2, c2, out):
-        for i in range(n):
-            at = slice(i * BLK, (i + 1) * BLK)
-            out[i, :, :BLK] = k1[:, at] + c1[:, at]
-            out[i, :, BLK:] = k2[:, at] + c2[:, at]
-
-    return call(body, arr(n, rows, 2 * BLK), keep_one, came_one, keep_two, came_two)
+    rows, _ = keep_one.shape
+    half = rows // 2
+
+    def body(k1, c1, k2, c2, own, plus, minus, upper, lower):
+        for d, outs in ((0, ((own, 0, rows),)), (1, ((plus, 0, rows),)), (3, ((minus, 0, rows),)),
+                        (2, ((upper, 0, half), (lower, half, half)))):
+            at = pl.ds(place("y", d, BLK), BLK)
+            for out, first, count in outs:
+                r = pl.ds(first, count)
+                out[:, :BLK] = k1[r, at] + c1[r, at]
+                out[:, BLK:] = k2[r, at] + c2[r, at]
+
+    shapes = [arr(rows, 2 * BLK)] * 3 + [arr(half, 2 * BLK)] * 2
+    return call(body, shapes, keep_one, came_one, keep_two, came_two)
+
+
+def relayed(plus, minus, from_minus, from_plus):
+    rows, cols = plus.shape
+    half = rows // 2
+
+    def body(p, m, t, b, p_out, m_out):
+        p_out[:half] = p[:half] + t[...]
+        p_out[half:] = p[half:]
+        m_out[:half] = m[:half]
+        m_out[half:] = m[half:] + b[...]
+
+    return call(body, [arr(rows, cols)] * 2, plus, minus, from_minus, from_plus)
+
+
+def summed_over_y(keep_one, came_one, keep_two, came_two):
+    own, plus, minus, upper, lower = by_column(keep_one, came_one, keep_two, came_two)
+    plus, minus = relayed(plus, minus, shifted(upper, "y", 1), shifted(lower, "y", -1))
+    return own, shifted(plus, "y", 1), shifted(minus, "y", -1)
 
 
 def contract(parts, beside):
-    n, rows, cols = parts.shape
+    rows, cols = parts[0].shape
     span, depth = beside[0].shape
     width = depth // 2
     half = 3 * width // 2
 
-    def body(ins, *refs):
-        total, keep, send, terms, left = refs[n:]
-        for d in range(n):
+    def body(a, b, c, *refs):
+        total, keep, send, terms, left = refs[4:]
+        for d in range(4):
             left[pl.ds(place("y", -d, span), span), :] = refs[d][...]
-        v = ins[0]
-        for i in range(1, n):
-            v = v + ins[i]
+        v = a[...] + (b[...] + c[...])
         total[...] = v
         one = halves(v[:, :BLK])
         two = halves(v[:, BLK:])
@@ -207,7 +251,7 @@
 
     shapes = [arr(rows, cols)] + [arr(half, BLK)] * 2
     return call(
-        body, shapes, parts, *beside, scratch=[pltpu.VMEM((2 * half, BLK), F32), pltpu.VMEM((rows, depth), F32)]
+        body, shapes, *parts, *beside, scratch=[pltpu.VMEM((2 * half, BLK), F32), pltpu.VMEM((rows, depth), F32)]
     )
 
 
@@ -219,18 +263,26 @@
     lax.fori_loop(0, cols // wide, step, 0)
 
 
-def gram(lower):
-    side = lower.shape[0]
-
-    def body(ref, out):
-        whole = halves(ref[...])
-
-        def part(at):
-            out[:, at] = dot3(whole, halves(ref[:, at]), ((0,), (0,)))
-
-        in_columns(side, 256, part)
-
-    return call(body, arr(side, side), lower)
+def grams(lower_one, lower_two):
+    side = lower_one.shape[0]
+    wide = 256
+
+    def body(one, two, g1, g2, both, out):
+        both[0] = one[...]
+        both[1] = two[...]
+
+        def step(i, carry):
+            which = lax.shift_right_logical(i, 1)
+            at = pl.ds(pl.multiple_of(lax.rem(i, 2) * wide, wide), wide)
+            out[which, :, at] = dot3(halves(both[which]), halves(both[which, :, at]), ((0,), (0,)))
+            return carry
+
+        lax.fori_loop(0, 2 * side // wide, step, 0)
+        g1[...] = out[0]
+        g2[...] = out[1]
+
+    scratch = [pltpu.VMEM((2, side, side), F32)] * 2
+    return call(body, [arr(side, side)] * 2, lower_one, lower_two, scratch=scratch)
 
 
 def finish(mine, other, gram_one, gram_two, upper):
@@ -241,10 +293,13 @@
     def body(own, far, g1, g2, u_ref, d1_ref, c_ref, d2_ref, terms):
         k = lax.axis_index("k")
         for ref, core in ((own, k), (far, 1 - k)):
-            for x in range(4):
+            def put(x, carry, ref=ref, core=core):
                 at = pl.ds(pl.multiple_of(core * half + x * rows, rows), rows)
                 for y in range(4):
                     terms[at, y * cols : (y + 1) * cols] = ref[4 * x + y]
+                return carry
+
+            lax.fori_loop(0, 4, put, 0)
         d1_ref[...] = g1[...] + terms[:side, :]
         c_ref[...] = terms[side : 2 * side, :].T
 
@@ -276,7 +331,7 @@
 
 
 def product(left, right):
-    return jnp.dot(left, right, precision=lax.Precision.HIGHEST, preferred_element_type=F32)
+    return jnp.dot(left, right, precision=lax.Precision.HIGH, preferred_element_type=F32)
 
 
 def owners():
@@ -292,22 +347,25 @@
 
 
 def at_z(d):
-    return lambda b: (jnp.int32(b), lax.rem(lax.axis_index("z") + d + 8, 8))
+    return lambda b: (b, lax.rem(lax.axis_index("z") + d + 8, 8))
 
 
 def at_x(d, first):
-    return lambda b: (lax.rem(lax.axis_index("x") + d + 4, 4), jnp.int32(first + b))
+    return lambda b: (lax.rem(lax.axis_index("x") + d + 4, 4), first + b)
 
 
 def inverted(inverse_pool, panel_one, panel_two, upper_two, lower_one, lower_two, list_one, list_two):
     span, width = panel_one.shape
-    both, masked_one, masked_two, keep_one, keep_two = masks(list_one, list_two, panel_one, panel_two)
-    moved_two = lax.ppermute(masked_two, ALL, owners())
-    moved_one = lax.ppermute(masked_one, ALL, owners())
+    moved_two = lax.ppermute(panel_two, ALL, owners())
+    moved_one = lax.ppermute(panel_one, ALL, owners())
+    both, keep_one, keep_two = masks(list_one, list_two, panel_one, panel_two)
     tile_hi, tile_lo = split_tile(inverse_pool, span)
-    beside = spread(both, "y")
-    moved_one, moved_two, tile_hi, tile_lo, beside = lax.optimization_barrier(
-        (moved_one, moved_two, tile_hi, tile_lo, beside)
+    live_one, live_two = column_masks(list_one, list_two, inverse_pool.shape[1])
+    beside = [both]
+    for d in range(1, 4):
+        beside.append(shifted(both, "y", d))
+    moved_one, moved_two, tile_hi, tile_lo, live_one, live_two = lax.optimization_barrier(
+        (moved_one, moved_two, tile_hi, tile_lo, live_one, live_two)
     )
 
     fans = spread(moved_one, "x")
@@ -328,16 +386,16 @@
     upper_far = shifted(upper_down, "x", -1)
     lower_far = shifted(lower_up, "x", 1)
 
-    chunks_one = [(strip, 0, at_z(0))]
+    chunks_one = [(strip, at_z(0))]
     up = down = strip
     for s in range(1, 5):
         up = shifted(up, "z", 1)
-        chunks_one.append((up, 0, at_z(-s)))
+        chunks_one.append((up, at_z(-s)))
         if s < 4:
             down = shifted(down, "z", -1)
-            chunks_one.append((down, 0, at_z(s)))
+            chunks_one.append((down, at_z(s)))
     chunks_two = [
-        (v, 0, at_x(d, first))
+        (v, at_x(d, first))
         for v, d, first in (
             (upper, 0, 0),
             (lower, 0, 4),
@@ -350,11 +408,11 @@
         )
     ]
 
-    keep1, send1 = multiply(tile_hi, tile_lo, chunks_one, width, span)
+    keep1, send1 = multiply(tile_hi, tile_lo, live_one, chunks_one, width, span)
     came1 = crossed(send1, "k", 1)
-    keep2, send2 = multiply(tile_hi, tile_lo, chunks_two, width, span)
+    keep2, send2 = multiply(tile_hi, tile_lo, live_two, chunks_two, width, span)
     came2 = crossed(send2, "k", 1)
-    parts = traded(by_column(keep1, came1, keep2, came2), "y")
+    parts = summed_over_y(keep1, came1, keep2, came2)
     total, keep, send = contract(parts, beside)
 
     terms = keep + crossed(send, "k", 1)
@@ -363,9 +421,10 @@
     for mask in (1, 2, 4):
         terms = terms + crossed(terms, "z", mask)
         if mask == 1:
-            terms, gram_one = lax.optimization_barrier((terms, gram(lower_one)))
+            gram_one, gram_two = grams(lower_one, lower_two)
+            terms, gram_one = lax.optimization_barrier((terms, gram_one))
         if mask == 2:
-            terms, lines, gram_two = lax.optimization_barrier((terms, lines, gram(lower_two)))
+            terms, lines = lax.optimization_barrier((terms, lines))
     mine = traded(jnp.broadcast_to(terms, (16, *terms.shape)), ("x", "y"))
     other = crossed(mine, "k", 1)
     first_diag, second_coupling, second_diag = finish(mine, other, gram_one, gram_two, upper_two)

time: 223 us -> 226 us (1.013)
  blocking collectives: 52.8 us -> 33.8 us
  waiting for transfers between devices: 53 us -> 60.8 us
  Pallas kernels: 42.3 us -> 49.1 us
  starting transfers between devices: 66.1 us -> 72.6 us
    all_to_all x3 -> x2, blocking collectives: 52.8 us -> 33.8 us  [traded(): return lax.all_to_all(v, axis, split_axis=0, concat_axis=0, tiled=True)]
    ppermute x26 -> x30, starting transfers between devices: 30.5 us -> 38.1 us  [shifted(): return lax.ppermute(v, axis, [(i, (i + by) % n) for i in range(n)])]
    pallas_call x11 -> x12, Pallas kernels: 42.3 us -> 49.1 us  [call(): pl.pallas_call(body, out_shape=out_shapes, in_specs=[whole] * len(args),...]
    ppermute x26 -> x30, waiting for transfers between devices: 41.1 us -> 45.3 us  [shifted(): return lax.ppermute(v, axis, [(i, (i + by) % n) for i in range(n)])]
    ppermute x7, waiting for transfers between devices: 11.9 us -> 15.5 us  [crossed(): return lax.ppermute(v, axis, [(i, i ^ mask) for i in range(SIZES[axis])])]
    ppermute x7, starting transfers between devices: 19.4 us -> 16.3 us  [crossed(): return lax.ppermute(v, axis, [(i, i ^ mask) for i in range(SIZES[axis])])]
    unnamed x69 -> x77, local copies, waits for them, and re-layouts: 4.17 us -> 5.52 us
  transfers between devices with their start and end apart: 36 -> 40, of which waited for: 15 -> 17; matrix products, arithmetic and copies ran while one was open for 1% -> 1% of each run, Pallas kernels for 11% -> 15%
where the time goes in v2:
time: 226 us; the launch traced here: 225 us
  starting transfers between devices  72.6 us (32%)
  waiting for transfers between devices  60.8 us (27%)
  Pallas kernels  49.1 us (22%)
  blocking collectives  33.8 us (15%)
  local copies, waits for them, and re-layouts  5.67 us (3%)
    pallas_call x12, Pallas kernels, call(): pl.pallas_call(body, out_shape=out_shapes, in_specs=[whole] * len(args),...  49.1 us
    ppermute x30, waiting for transfers between devices, shifted(): return lax.ppermute(v, axis, [(i, (i + by) % n) for i in range(n)])  45.3 us
    ppermute x30, starting transfers between devices, shifted(): return lax.ppermute(v, axis, [(i, (i + by) % n) for i in range(n)])  38.1 us
    all_to_all x2, blocking collectives, traded(): return lax.all_to_all(v, axis, split_axis=0, concat_axis=0, tiled=True)  33.8 us
    ppermute x7, starting transfers between devices, crossed(): return lax.ppermute(v, axis, [(i, i ^ mask) for i in range(SIZES[axis])])  16.3 us
    ppermute x7, waiting for transfers between devices, crossed(): return lax.ppermute(v, axis, [(i, i ^ mask) for i in range(SIZES[axis])])  15.5 us
    ppermute x1, starting transfers between devices, inverted(): moved_one = lax.ppermute(panel_one, ALL, owners())  9.31 us
    unnamed x77, local copies, waits for them, and re-layouts  5.52 us
  transfers between devices with their start and end apart: 40, of which 17 were waited for; matrix products, arithmetic and copies ran while one was open for 1% of the time, Pallas kernels for 15%

profile of v2, /device:TPU:1, one launch (start us, length us, event | category | flops | bytes accessed | tf_op | source)
XLA Modules:
  0.0 225.3 jit_solution(14211825418492860736)
XLA Ops:
  0.6 9.3 %collective-permute-start = (f32[48,512]{1,0:T(8,128)}, f32[48,512]{1,0:T(8,128)S(1)}, u32[]{:S(2)}, u32[]{:S(2)}) collective-permute-start(f32[48,512]{1,0:T(8,128)} %one.2), channel_id=1, source_target_pairs={{0,176},{1,48},{2,184},{3,56},{4,112},{5,240},{6,120},{7,248},{8,1... | collective-permute-start | bytes 294920 | tf_op jit(solution)/shard_map/ppermute | solution.py:360
  9.9 4.4 %collective-permute-start.1 = (f32[48,512]{1,0:T(8,128)}, f32[48,512]{1,0:T(8,128)S(1)}, u32[]{:S(2)}, u32[]{:S(2)}) collective-permute-start(f32[48,512]{1,0:T(8,128)} %two.2), channel_id=1, source_target_pairs={{0,176},{1,48},{2,184},{3,56},{4,112},{5,240},{6,120},{7,248},{8,1... | collective-permute-start | bytes 294920 | tf_op jit(solution)/shard_map/ppermute | solution.py:359
  14.3 3.4 %shard_map.120 = (bf16[384,1536]{1,0:T(8,128)(2,1)}, bf16[384,1536]{1,0:T(8,128)(2,1)}) custom-call(f32[384,1536]{1,0:T(8,128)} %a.1), custom_call_target="tpu_custom_call" | custom-call | tf_op jit(solution)/shard_map/pallas_call | solution.py:20
  17.7 4.0 %shard_map.121 = (f32[1536,128]{1,0:T(8,128)}, f32[1536,128]{1,0:T(8,128)}) custom-call(s32[1,72]{1,0:T(1,128)} %bitcast.17, s32[1,48]{1,0:T(1,128)} %bitcast.19), custom_call_target="tpu_custom_call" | custom-call | tf_op jit(solution)/shard_map/pallas_call | solution.py:20
  26.3 4.7 %collective-permute-start.3 = (f32[48,512]{1,0:T(8,128)S(1)}, f32[48,512]{1,0:T(8,128)S(1)}, u32[]{:S(2)}, u32[]{:S(2)}) collective-permute-start(f32[48,512]{1,0:T(8,128)S(1)} %collective-permute-done.refs_0_), channel_id=1, source_target_pairs={{0,128},{64,192},{128,0},{192,64},{1,129},{65,193},{129,1},{193,65... | collective-permute-start | bytes 294920 | tf_op jit(solution)/shard_map/ppermute | solution.py:47
  40.7 6.6 %collective-permute-done.9.refs_4_ = f32[192,512]{1,0:T(8,128)S(1)} collective-permute-done((f32[192,512]{1,0:T(8,128)}, f32[192,512]{1,0:T(8,128)S(1)}, u32[]{:S(2)}, u32[]{:S(2)}) %collective-permute-start.9) | collective-permute-done | bytes 393248 | tf_op jit(solution)/shard_map/ppermute | solution.py:47
  50.0 7.6 %collective-permute-done.17.refs_3_ = f32[48,512]{1,0:T(8,128)S(1)} collective-permute-done((f32[48,512]{1,0:T(8,128)S(1)}, f32[48,512]{1,0:T(8,128)S(1)}, u32[]{:S(2)}, u32[]{:S(2)}) %collective-permute-start.17) | collective-permute-done | bytes 98336 | tf_op jit(solution)/shard_map/ppermute | solution.py:47
  57.6 4.9 %collective-permute-done.18.refs_4_ = f32[48,512]{1,0:T(8,128)S(1)} collective-permute-done((f32[48,512]{1,0:T(8,128)S(1)}, f32[48,512]{1,0:T(8,128)S(1)}, u32[]{:S(2)}, u32[]{:S(2)}) %collective-permute-start.18) | collective-permute-done | bytes 98336 | tf_op jit(solution)/shard_map/ppermute | solution.py:47
  69.5 3.5 %collective-permute-done.22.refs_7_ = f32[192,512]{1,0:T(8,128)S(1)} collective-permute-done((f32[192,512]{1,0:T(8,128)}, f32[192,512]{1,0:T(8,128)S(1)}, u32[]{:S(2)}, u32[]{:S(2)}) %collective-permute-start.22) | collective-permute-done | bytes 393248 | tf_op jit(solution)/shard_map/ppermute | solution.py:47
  76.0 7.0 %collective-permute-done.20.refs_5_ = f32[192,512]{1,0:T(8,128)S(1)} collective-permute-done((f32[192,512]{1,0:T(8,128)}, f32[192,512]{1,0:T(8,128)S(1)}, u32[]{:S(2)}, u32[]{:S(2)}) %collective-permute-start.20) | collective-permute-done | bytes 393248 | tf_op jit(solution)/shard_map/ppermute | solution.py:47
  84.6 3.9 %collective-permute-done.24.refs_9_ = f32[192,512]{1,0:T(8,128)S(1)} collective-permute-done((f32[192,512]{1,0:T(8,128)S(1)}, f32[192,512]{1,0:T(8,128)S(1)}, u32[]{:S(2)}, u32[]{:S(2)}) %collective-permute-start.24) | collective-permute-done | bytes 393248 | tf_op jit(solution)/shard_map/ppermute | solution.py:47
  89.3 3.6 %collective-permute-done.25.refs_10_ = f32[192,512]{1,0:T(8,128)} collective-permute-done((f32[192,512]{1,0:T(8,128)S(1)}, f32[192,512]{1,0:T(8,128)}, u32[]{:S(2)}, u32[]{:S(2)}) %collective-permute-start.25) | collective-permute-done | bytes 393248 | tf_op jit(solution)/shard_map/ppermute | solution.py:47
  92.9 7.2 %shard_map.125 = (f32[192,512]{1,0:T(8,128)}, f32[192,512]{1,0:T(8,128)}) custom-call(bf16[384,1536]{1,0:T(8,128)(2,1)} %get-tuple-element.56.refs_0_, bf16[384,1536]{1,0:T(8,128)(2,1)} %get-tuple-element.57.refs_1_, f32[1536,128]{1,0:T(8,128)} %get-tuple-element.67.refs_2_, f32[192,512]{1,0:T(8,128)} %get-tuple-element.72.refs_3_, ...), custom_call_target="tpu_custom_call" | custom-call | tf_op jit(solution)/shard_map/pallas_call | solution.py:20
  100.2 7.4 %collective-permute-start.26 = (f32[192,512]{1,0:T(8,128)}, f32[192,512]{1,0:T(8,128)S(1)}, u32[]{:S(2)}, u32[]{:S(2)}) collective-permute-start(f32[192,512]{1,0:T(8,128)} %get-tuple-element.75), channel_id=1, source_target_pairs={{0,1},{1,0},{2,3},{3,2},{4,5},{5,4},{6,7},{7,6},{8,9},{9,8},{10,11... | collective-permute-start | bytes 1179656 | tf_op jit(solution)/shard_map/ppermute | solution.py:51
  108.3 7.3 %shard_map.123 = (f32[192,512]{1,0:T(8,128)}, f32[192,512]{1,0:T(8,128)}) custom-call(bf16[384,1536]{1,0:T(8,128)(2,1)} %get-tuple-element.56.refs_0_, bf16[384,1536]{1,0:T(8,128)(2,1)} %get-tuple-element.57.refs_1_, f32[1536,128]{1,0:T(8,128)} %get-tuple-element.58.refs_2_, f32[192,512]{1,0:T(8,128)} %shard_map.122.refs_3_, f32[192,512]{1,0:T(8,128)} %copy-done.3, ...), custom_call_target="tpu_custom_call" | custom-call | tf_op jit(solution)/shard_map/pallas_call | solution.py:20
  138.8 4.2 %collective-permute-done.29.b = f32[192,256]{1,0:T(8,128)S(1)} collective-permute-done((f32[192,256]{1,0:T(8,128)}, f32[192,256]{1,0:T(8,128)S(1)}, u32[]{:S(2)}, u32[]{:S(2)}) %collective-permute-start.29) | collective-permute-done | bytes 196640 | tf_op jit(solution)/shard_map/ppermute | solution.py:47
  151.0 10.2 %all_to_all.15 = f32[4,192,128]{2,1,0:T(8,128)S(1)} all-to-all(f32[4,192,128]{2,1,0:T(8,128)S(1)} %bitcast.16), channel_id=1, replica_groups=mesh['x'=4,'z'=8,'y'=4,'k'=2] {'x'}, dimensions={0} | all-to-all | bytes 786432 | tf_op jit(solution)/shard_map/all_to_all | solution.py:55
  161.3 4.5 %all-to-all-start.1 = ((f32[4,48,256]{2,1,0:T(8,128)}), f32[4,48,256]{2,1,0:T(8,128)S(1)}, u32[]{:S(2)}, u32[]{:S(2)}) async-start(f32[4,48,256]{2,1,0:T(8,128)} %bitcast.3), calls=%async_computation.1 | async-start | bytes 393216 | tf_op jit(solution)/shard_map/all_to_all | solution.py:55
  165.8 5.8 %shard_map.129 = (f32[512,512]{1,0:T(8,128)}, f32[512,512]{1,0:T(8,128)}) custom-call(f32[512,512]{1,0:T(8,128)} %one.3, f32[512,512]{1,0:T(8,128)} %two.3), custom_call_target="tpu_custom_call" | custom-call | tf_op jit(solution)/shard_map/pallas_call | solution.py:20
  171.7 4.4 %collective-permute-done.36 = f32[192,128]{1,0:T(8,128)S(1)} collective-permute-done((f32[192,128]{1,0:T(8,128)S(1)}, f32[192,128]{1,0:T(8,128)S(1)}, u32[]{:S(2)}, u32[]{:S(2)}) %collective-permute-start.36) | collective-permute-done | bytes 98336 | tf_op jit(solution)/shard_map/ppermute | solution.py:51
  178.8 5.9 %collective-permute-done.37 = f32[192,128]{1,0:T(8,128)S(1)} collective-permute-done((f32[192,128]{1,0:T(8,128)S(1)}, f32[192,128]{1,0:T(8,128)S(1)}, u32[]{:S(2)}, u32[]{:S(2)}) %collective-permute-start.37) | collective-permute-done | bytes 98336 | tf_op jit(solution)/shard_map/ppermute | solution.py:51
  184.9 23.6 %all_to_all.16.own = f32[16,192,128]{2,1,0:T(8,128)S(1)} all-to-all(f32[16,192,128]{2,1,0:T(8,128)S(1)} %broadcast_in_dim.13), channel_id=1, replica_groups=mesh['x'=4,'z'=8,'y'=4,'k'=2] {'x','y'}, dimensions={0} | all-to-all | bytes 3145728 | tf_op jit(solution)/shard_map/all_to_all | solution.py:55
  208.5 4.7 %collective-permute-start.38 = (f32[16,192,128]{2,1,0:T(8,128)S(1)}, f32[16,192,128]{2,1,0:T(8,128)S(1)}, u32[]{:S(2)}, u32[]{:S(2)}) collective-permute-start(f32[16,192,128]{2,1,0:T(8,128)S(1)} %all_to_all.16.own), channel_id=1, source_target_pairs={{0,1},{1,0},{2,3},{3,2},{4,5},{5,4},{6,7},{7,6},{8,9},{9,8},{10,11... | collective-permute-start | bytes 4718600 | tf_op jit(solution)/shard_map/ppermute | solution.py:51
  217.4 7.9 %shard_map.130 = (f32[512,512]{1,0:T(8,128)}, f32[512,512]{1,0:T(8,128)}, f32[512,512]{1,0:T(8,128)}) custom-call(f32[16,192,128]{2,1,0:T(8,128)} %copy-done, f32[16,192,128]{2,1,0:T(8,128)} %copy-done.2, f32[512,512]{1,0:T(8,128)} %get-tuple-element.91.g1, f32[512,512]{1,0:T(8,128)} %get-tuple-element.92.g2, f32[512,512]{1,0:T(8,128)} %u_ref.1), custom_call_target="tpu_custom_call" | custom-call | tf_op jit(solution)/shard_map/pallas_call | solution.py:20
  (156 shorter events, 68.3 us)
Async XLA Ops:
  0.6 21.1 %collective-permute-start = (f32[48,512]{1,0:T(8,128)}, f32[48,512]{1,0:T(8,128)S(1)}, u32[]{:S(2)}, u32[]{:S(2)}) collective-permute-start(f32[48,512]{1,0:T(8,128)} %one.2), channel_id=1, source_target_pairs={{0,176},{1,48},{2,184},{3,56},{4,112},{5,240},{6,120},{7,248},{8,1... | collective-permute-start | bytes 294920 | tf_op jit(solution)/shard_map/ppermute | solution.py:360
  9.9 11.8 %collective-permute-start.1 = (f32[48,512]{1,0:T(8,128)}, f32[48,512]{1,0:T(8,128)S(1)}, u32[]{:S(2)}, u32[]{:S(2)}) collective-permute-start(f32[48,512]{1,0:T(8,128)} %two.2), channel_id=1, source_target_pairs={{0,176},{1,48},{2,184},{3,56},{4,112},{5,240},{6,120},{7,248},{8,1... | collective-permute-start | bytes 294920 | tf_op jit(solution)/shard_map/ppermute | solution.py:359
  21.8 9.2 %collective-permute-start.5 = (f32[48,512]{1,0:T(8,128)S(1)}, f32[48,512]{1,0:T(8,128)S(1)}, u32[]{:S(2)}, u32[]{:S(2)}) collective-permute-start(f32[48,512]{1,0:T(8,128)S(1)} %collective-permute-done.1.refs_0_), channel_id=1, source_target_pairs={{0,8},{8,16},{16,24},{24,32},{32,40},{40,48},{48,56},{56,0},{1,9},... | collective-permute-start | bytes 294920 | tf_op jit(solution)/shard_map/ppermute | solution.py:47
  24.5 9.2 %collective-permute-start.2 = (f32[48,512]{1,0:T(8,128)S(1)}, f32[48,512]{1,0:T(8,128)S(1)}, u32[]{:S(2)}, u32[]{:S(2)}) collective-permute-start(f32[48,512]{1,0:T(8,128)S(1)} %collective-permute-done.refs_0_), channel_id=1, source_target_pairs={{0,64},{64,128},{128,192},{192,0},{1,65},{65,129},{129,193},{193,1... | collective-permute-start | bytes 294920 | tf_op jit(solution)/shard_map/ppermute | solution.py:47
  38.0 9.3 %collective-permute-start.9 = (f32[192,512]{1,0:T(8,128)}, f32[192,512]{1,0:T(8,128)S(1)}, u32[]{:S(2)}, u32[]{:S(2)}) collective-permute-start(f32[192,512]{1,0:T(8,128)} %shard_map.122.refs_3_), channel_id=1, source_target_pairs={{0,8},{8,16},{16,24},{24,32},{32,40},{40,48},{48,56},{56,0},{1,9},... | collective-permute-start | bytes 1179656 | tf_op jit(solution)/shard_map/ppermute | solution.py:47
  38.0 29.9 %collective-permute-start.10 = (f32[192,512]{1,0:T(8,128)}, f32[192,512]{1,0:T(8,128)S(1)}, u32[]{:S(2)}, u32[]{:S(2)}) collective-permute-start(f32[192,512]{1,0:T(8,128)} %shard_map.122.refs_3_), channel_id=1, source_target_pairs={{0,56},{8,0},{16,8},{24,16},{32,24},{40,32},{48,40},{56,48},{1,57}... | collective-permute-start | bytes 1179656 | tf_op jit(solution)/shard_map/ppermute | solution.py:47
  47.3 20.8 %collective-permute-start.11 = (f32[192,512]{1,0:T(8,128)S(1)}, f32[192,512]{1,0:T(8,128)S(1)}, u32[]{:S(2)}, u32[]{:S(2)}) collective-permute-start(f32[192,512]{1,0:T(8,128)S(1)} %collective-permute-done.9.refs_4_), channel_id=1, source_target_pairs={{0,8},{8,16},{16,24},{24,32},{32,40},{40,48},{48,56},{56,0},{1,9},... | collective-permute-start | bytes 1179656 | tf_op jit(solution)/shard_map/ppermute | solution.py:47
  47.3 10.3 %collective-permute-start.17 = (f32[48,512]{1,0:T(8,128)S(1)}, f32[48,512]{1,0:T(8,128)S(1)}, u32[]{:S(2)}, u32[]{:S(2)}) collective-permute-start(f32[48,512]{1,0:T(8,128)S(1)} %collective-permute-done.6.refs_2_), channel_id=1, source_target_pairs={{0,8},{8,16},{16,24},{24,32},{32,40},{40,48},{48,56},{56,0},{1,9},... | collective-permute-start | bytes 294920 | tf_op jit(solution)/shard_map/ppermute | solution.py:47
  47.3 10.3 %collective-permute-start.19 = (f32[48,512]{1,0:T(8,128)S(1)}, f32[48,512]{1,0:T(8,128)S(1)}, u32[]{:S(2)}, u32[]{:S(2)}) collective-permute-start(f32[48,512]{1,0:T(8,128)S(1)} %collective-permute-done.8.refs_6_), channel_id=1, source_target_pairs={{0,56},{8,0},{16,8},{24,16},{32,24},{40,32},{48,40},{56,48},{1,57}... | collective-permute-start | bytes 294920 | tf_op jit(solution)/shard_map/ppermute | solution.py:47
  67.9 15.2 %collective-permute-start.20 = (f32[192,512]{1,0:T(8,128)}, f32[192,512]{1,0:T(8,128)S(1)}, u32[]{:S(2)}, u32[]{:S(2)}) collective-permute-start(f32[192,512]{1,0:T(8,128)} %get-tuple-element.72.refs_3_), channel_id=1, source_target_pairs={{0,64},{64,128},{128,192},{192,0},{1,65},{65,129},{129,193},{193,1... | collective-permute-start | bytes 1179656 | tf_op jit(solution)/shard_map/ppermute | solution.py:47
  67.9 15.2 %collective-permute-start.12 = (f32[192,512]{1,0:T(8,128)S(1)}, f32[192,512]{1,0:T(8,128)S(1)}, u32[]{:S(2)}, u32[]{:S(2)}) collective-permute-start(f32[192,512]{1,0:T(8,128)S(1)} %collective-permute-done.10.refs_5_), channel_id=1, source_target_pairs={{0,56},{8,0},{16,8},{24,16},{32,24},{40,32},{48,40},{56,48},{1,57}... | collective-permute-start | bytes 1179656 | tf_op jit(solution)/shard_map/ppermute | solution.py:47
  68.1 15.1 %collective-permute-start.13 = (f32[192,512]{1,0:T(8,128)S(1)}, f32[192,512]{1,0:T(8,128)S(1)}, u32[]{:S(2)}, u32[]{:S(2)}) collective-permute-start(f32[192,512]{1,0:T(8,128)S(1)} %collective-permute-done.11.refs_6_), channel_id=1, source_target_pairs={{0,8},{8,16},{16,24},{24,32},{32,40},{40,48},{48,56},{56,0},{1,9},... | collective-permute-start | bytes 1179656 | tf_op jit(solution)/shard_map/ppermute | solution.py:47
  72.9 11.7 %collective-permute-start.23 = (f32[192,512]{1,0:T(8,128)}, f32[192,512]{1,0:T(8,128)S(1)}, u32[]{:S(2)}, u32[]{:S(2)}) collective-permute-start(f32[192,512]{1,0:T(8,128)} %get-tuple-element.73.refs_4_), channel_id=1, source_target_pairs={{0,192},{64,0},{128,64},{192,128},{1,193},{65,1},{129,65},{193,129... | collective-permute-start | bytes 1179656 | tf_op jit(solution)/shard_map/ppermute | solution.py:47
  75.9 12.6 %collective-permute-start.24 = (f32[192,512]{1,0:T(8,128)S(1)}, f32[192,512]{1,0:T(8,128)S(1)}, u32[]{:S(2)}, u32[]{:S(2)}) collective-permute-start(f32[192,512]{1,0:T(8,128)S(1)} %collective-permute-done.22.refs_7_), channel_id=1, source_target_pairs={{0,192},{64,0},{128,64},{192,128},{1,193},{65,1},{129,65},{193,129... | collective-permute-start | bytes 1179656 | tf_op jit(solution)/shard_map/ppermute | solution.py:47
  83.1 9.8 %collective-permute-start.25 = (f32[192,512]{1,0:T(8,128)S(1)}, f32[192,512]{1,0:T(8,128)}, u32[]{:S(2)}, u32[]{:S(2)}) collective-permute-start(f32[192,512]{1,0:T(8,128)S(1)} %collective-permute-done.21.refs_6_), channel_id=1, source_target_pairs={{0,64},{64,128},{128,192},{192,0},{1,65},{65,129},{129,193},{193,1... | collective-permute-start | bytes 1179656 | tf_op jit(solution)/shard_map/ppermute | solution.py:47
  83.1 24.5 %collective-permute-start.14 = (f32[192,512]{1,0:T(8,128)S(1)}, f32[192,512]{1,0:T(8,128)S(1)}, u32[]{:S(2)}, u32[]{:S(2)}) collective-permute-start(f32[192,512]{1,0:T(8,128)S(1)} %collective-permute-done.12.refs_7_), channel_id=1, source_target_pairs={{0,56},{8,0},{16,8},{24,16},{32,24},{40,32},{48,40},{56,48},{1,57}... | collective-permute-start | bytes 1179656 | tf_op jit(solution)/shard_map/ppermute | solution.py:47
  83.2 24.4 %collective-permute-start.15 = (f32[192,512]{1,0:T(8,128)S(1)}, f32[192,512]{1,0:T(8,128)}, u32[]{:S(2)}, u32[]{:S(2)}) collective-permute-start(f32[192,512]{1,0:T(8,128)S(1)} %collective-permute-done.13.refs_8_), channel_id=1, source_target_pairs={{0,8},{8,16},{16,24},{24,32},{32,40},{40,48},{48,56},{56,0},{1,9},... | collective-permute-start | bytes 1179656 | tf_op jit(solution)/shard_map/ppermute | solution.py:47
  100.2 15.5 %collective-permute-start.26 = (f32[192,512]{1,0:T(8,128)}, f32[192,512]{1,0:T(8,128)S(1)}, u32[]{:S(2)}, u32[]{:S(2)}) collective-permute-start(f32[192,512]{1,0:T(8,128)} %get-tuple-element.75), channel_id=1, source_target_pairs={{0,1},{1,0},{2,3},{3,2},{4,5},{5,4},{6,7},{7,6},{8,9},{9,8},{10,11... | collective-permute-start | bytes 1179656 | tf_op jit(solution)/shard_map/ppermute | solution.py:51
  120.7 11.2 %collective-permute-start.27 = (f32[96,256]{1,0:T(8,128)}, f32[96,256]{1,0:T(8,128)S(1)}, u32[]{:S(2)}, u32[]{:S(2)}) collective-permute-start(f32[96,256]{1,0:T(8,128)} %get-tuple-element.79), channel_id=1, source_target_pairs={{0,2},{2,4},{4,6},{6,0},{1,3},{3,5},{5,7},{7,1},{8,10},{10,12},{12... | collective-permute-start | bytes 294920 | tf_op jit(solution)/shard_map/ppermute | solution.py:47
  121.2 10.6 %collective-permute-start.28 = (f32[96,256]{1,0:T(8,128)}, f32[96,256]{1,0:T(8,128)S(1)}, u32[]{:S(2)}, u32[]{:S(2)}) collective-permute-start(f32[96,256]{1,0:T(8,128)} %get-tuple-element.80), channel_id=1, source_target_pairs={{0,6},{2,0},{4,2},{6,4},{1,7},{3,1},{5,3},{7,5},{8,14},{10,8},{12,... | collective-permute-start | bytes 294920 | tf_op jit(solution)/shard_map/ppermute | solution.py:47
  125.2 11.9 %collective-permute-start.31 = (f32[48,1024]{1,0:T(8,128)}, f32[48,1024]{1,0:T(8,128)S(1)}, u32[]{:S(2)}, u32[]{:S(2)}) collective-permute-start(f32[48,1024]{1,0:T(8,128)} %get-tuple-element.83.refs_0_), channel_id=1, source_target_pairs={{0,2},{2,4},{4,6},{6,0},{1,3},{3,5},{5,7},{7,1},{8,10},{10,12},{12... | collective-permute-start | bytes 589832 | tf_op jit(solution)/shard_map/ppermute | solution.py:47
  128.0 10.8 %collective-permute-start.32 = (f32[48,1024]{1,0:T(8,128)}, f32[48,1024]{1,0:T(8,128)S(1)}, u32[]{:S(2)}, u32[]{:S(2)}) collective-permute-start(f32[48,1024]{1,0:T(8,128)} %get-tuple-element.83.refs_0_), channel_id=1, source_target_pairs={{0,4},{2,6},{4,0},{6,2},{1,5},{3,7},{5,1},{7,3},{8,12},{10,14},{12... | collective-permute-start | bytes 589832 | tf_op jit(solution)/shard_map/ppermute | solution.py:47
  161.2 10.4 %collective-permute-start.35 = (f32[192,128]{1,0:T(8,128)S(1)}, f32[192,128]{1,0:T(8,128)S(1)}, u32[]{:S(2)}, u32[]{:S(2)}) collective-permute-start(f32[192,128]{1,0:T(8,128)S(1)} %reduce_sum.9), channel_id=1, source_target_pairs={{0,8},{8,0},{16,24},{24,16},{32,40},{40,32},{48,56},{56,48},{1,9},... | collective-permute-start | bytes 294920 | tf_op jit(solution)/shard_map/ppermute | solution.py:51
  161.3 14.8 %all-to-all-start.1 = ((f32[4,48,256]{2,1,0:T(8,128)}), f32[4,48,256]{2,1,0:T(8,128)S(1)}, u32[]{:S(2)}, u32[]{:S(2)}) async-start(f32[4,48,256]{2,1,0:T(8,128)} %bitcast.3), calls=%async_computation.1 | async-start | bytes 393216 | tf_op jit(solution)/shard_map/all_to_all | solution.py:55
  (54 other events, 617.3 us)

commit v3 on v2

--- a/solution.py
+++ b/solution.py
@@ -64,40 +64,24 @@
     return pl.multiple_of(lax.rem(lax.axis_index(axis) + (n + d) % n, n) * step, step)
 
 
-def live_at(listing, first, rows):
-    row = lax.broadcasted_iota(jnp.int32, (rows, listing.shape[1]), 0) + first
-    hits = jnp.where(lax.shift_right_logical(row, 7) == listing[...], 1.0, 0.0).astype(F32)
-    return jnp.max(hits, axis=1, keepdims=True)
-
-
 def masks(list_one, list_two, panel_one, panel_two):
     rows, cols = panel_one.shape
 
-    def body(one_list, two_list, one, two, both, keep1, keep2):
+    def body(one_list, two_list, one, two, both, out1, out2, keep1, keep2):
         index = lax.axis_index("x")
         for axis in ("z", "y", "k"):
             index = index * SIZES[axis] + lax.axis_index(axis)
-        for listing, panel, keep, at in ((one_list, one, keep1, 0), (two_list, two, keep2, cols)):
-            live = live_at(listing, index * rows, rows)
+        for listing, panel, out, keep, at in ((one_list, one, out1, keep1, 0), (two_list, two, out2, keep2, cols)):
+            row = lax.broadcasted_iota(jnp.int32, (rows, listing.shape[1]), 0) + index * rows
+            hits = jnp.where(lax.shift_right_logical(row, 7) == listing[...], 1.0, 0.0).astype(F32)
+            live = jnp.max(hits, axis=1, keepdims=True)
             keep[...] = jnp.broadcast_to(live, (rows, BLK))
-            both[:, at : at + cols] = live * panel[...]
-
-    shapes = [arr(rows, 2 * cols), arr(rows, BLK), arr(rows, BLK)]
+            v = live * panel[...]
+            out[...] = v
+            both[:, at : at + cols] = v
+
+    shapes = [arr(rows, 2 * cols)] + [arr(rows, cols)] * 2 + [arr(rows, BLK)] * 2
     return call(body, shapes, list_one[None], list_two[None], panel_one, panel_two)
-
-
-def column_masks(list_one, list_two, depth):
-    def body(one_list, two_list, live1, live2):
-        first = (lax.axis_index("y") * 2 + lax.axis_index("k")) * depth
-        for listing, out in ((one_list, live1), (two_list, live2)):
-            def put(i, carry, listing=listing, out=out):
-                at = pl.multiple_of(i * BLK, BLK)
-                out[pl.ds(at, BLK), :] = jnp.broadcast_to(live_at(listing, first + at, BLK), (BLK, BLK))
-                return carry
-
-            lax.fori_loop(0, depth // BLK, put, 0)
-
-    return call(body, [arr(depth, BLK)] * 2, list_one[None], list_two[None])
 
 
 def split_tile(tile, span):
@@ -152,26 +136,20 @@
     return lax.shift_right_logical(order, 1) * 8 + lax.rem(order, 2) * 2 + side
 
 
-def multiply(tile_hi, tile_lo, live, chunks, cols, span):
+def multiply(tile_hi, tile_lo, chunks, cols, span):
     rows, depth = tile_hi.shape
     m = len(chunks)
     wide = 256
 
     def body(*refs):
-        hi, lo, kept = refs[:3]
-        keep, send, b_hi, b_lo = refs[3 + m :]
-        for ref, (_, at_of) in zip(refs[3 : 3 + m], chunks):
-            def put(b, carry, ref=ref, at_of=at_of):
+        hi, lo = refs[0], refs[1]
+        keep, send, b_hi, b_lo = refs[2 + m :]
+        for ref, (_, column, at_of) in zip(refs[2 : 2 + m], chunks):
+            for b in range(ref.shape[0] // span):
+                h, l = halves(ref[b * span : (b + 1) * span, :])
                 at = pl.ds(pl.multiple_of(spot(*at_of(b)) * span, span), span)
-                rows_at = pl.ds(pl.multiple_of(b * span, span), span)
-                mask = kept[at, :]
-                for c in range(0, cols, BLK):
-                    h, l = halves(mask * ref[rows_at, c : c + BLK])
-                    b_hi[at, c : c + BLK] = h
-                    b_lo[at, c : c + BLK] = l
-                return carry
-
-            lax.fori_loop(0, ref.shape[0] // span, put, 0)
+                b_hi[at, column : column + ref.shape[1]] = h
+                b_lo[at, column : column + ref.shape[1]] = l
 
         def step(i, carry):
             at = pl.ds(pl.multiple_of(i * wide, wide), wide)
@@ -187,7 +165,6 @@
         [arr(rows // 2, cols)] * 2,
         tile_hi,
         tile_lo,
-        live,
         *[c[0] for c in chunks],
         scratch=[pltpu.VMEM((depth, cols), BF16)] * 2,
     )
@@ -356,16 +333,13 @@
 
 def inverted(inverse_pool, panel_one, panel_two, upper_two, lower_one, lower_two, list_one, list_two):
     span, width = panel_one.shape
-    moved_two = lax.ppermute(panel_two, ALL, owners())
-    moved_one = lax.ppermute(panel_one, ALL, owners())
-    both, keep_one, keep_two = masks(list_one, list_two, panel_one, panel_two)
+    both, masked_one, masked_two, keep_one, keep_two = masks(list_one, list_two, panel_one, panel_two)
+    moved_two = lax.ppermute(masked_two, ALL, owners())
+    moved_one = lax.ppermute(masked_one, ALL, owners())
     tile_hi, tile_lo = split_tile(inverse_pool, span)
-    live_one, live_two = column_masks(list_one, list_two, inverse_pool.shape[1])
-    beside = [both]
-    for d in range(1, 4):
-        beside.append(shifted(both, "y", d))
-    moved_one, moved_two, tile_hi, tile_lo, live_one, live_two = lax.optimization_barrier(
-        (moved_one, moved_two, tile_hi, tile_lo, live_one, live_two)
+    beside = spread(both, "y")
+    moved_one, moved_two, tile_hi, tile_lo, beside = lax.optimization_barrier(
+        (moved_one, moved_two, tile_hi, tile_lo, beside)
     )
 
     fans = spread(moved_one, "x")
@@ -386,16 +360,16 @@
     upper_far = shifted(upper_down, "x", -1)
     lower_far = shifted(lower_up, "x", 1)
 
-    chunks_one = [(strip, at_z(0))]
+    chunks_one = [(strip, 0, at_z(0))]
     up = down = strip
     for s in range(1, 5):
         up = shifted(up, "z", 1)
-        chunks_one.append((up, at_z(-s)))
+        chunks_one.append((up, 0, at_z(-s)))
         if s < 4:
             down = shifted(down, "z", -1)
-            chunks_one.append((down, at_z(s)))
+            chunks_one.append((down, 0, at_z(s)))
     chunks_two = [
-        (v, at_x(d, first))
+        (v, 0, at_x(d, first))
         for v, d, first in (
             (upper, 0, 0),
             (lower, 0, 4),
@@ -408,9 +382,9 @@
         )
     ]
 
-    keep1, send1 = multiply(tile_hi, tile_lo, live_one, chunks_one, width, span)
+    keep1, send1 = multiply(tile_hi, tile_lo, chunks_one, width, span)
     came1 = crossed(send1, "k", 1)
-    keep2, send2 = multiply(tile_hi, tile_lo, live_two, chunks_two, width, span)
+    keep2, send2 = multiply(tile_hi, tile_lo, chunks_two, width, span)
     came2 = crossed(send2, "k", 1)
     parts = summed_over_y(keep1, came1, keep2, came2)
     total, keep, send = contract(parts, beside)

time: 226 us -> 224 us (level)
  waiting for transfers between devices: 60.8 us -> 68.5 us
  Pallas kernels: 49.1 us -> 42.6 us
    ppermute x30, waiting for transfers between devices: 45.3 us -> 52 us  [shifted(): return lax.ppermute(v, axis, [(i, (i + by) % n) for i in range(n)])]
    pallas_call x12 -> x11, Pallas kernels: 49.1 us -> 42.6 us  [call(): pl.pallas_call(body, out_shape=out_shapes, in_specs=[whole] * len(args),...]
  transfers between devices with their start and end apart: 40 -> 40, of which waited for: 17 -> 18; matrix products, arithmetic and copies ran while one was open for 1% -> 1% of each run, Pallas kernels for 15% -> 10%
where the time goes in v3:
time: 224 us
  starting transfers between devices  71 us (32%)
  waiting for transfers between devices  68.5 us (31%)
  Pallas kernels  42.6 us (19%)
  blocking collectives  32.5 us (15%)
  local copies, waits for them, and re-layouts  5.75 us (3%)
    ppermute x30, waiting for transfers between devices, shifted(): return lax.ppermute(v, axis, [(i, (i + by) % n) for i in range(n)])  52 us
    pallas_call x11, Pallas kernels, call(): pl.pallas_call(body, out_shape=out_shapes, in_specs=[whole] * len(args),...  42.6 us
    ppermute x30, starting transfers between devices, shifted(): return lax.ppermute(v, axis, [(i, (i + by) % n) for i in range(n)])  35.9 us
    all_to_all x2, blocking collectives, traded(): return lax.all_to_all(v, axis, split_axis=0, concat_axis=0, tiled=True)  32.5 us
    ppermute x7, starting transfers between devices, crossed(): return lax.ppermute(v, axis, [(i, i ^ mask) for i in range(SIZES[axis])])  18.4 us
    ppermute x7, waiting for transfers between devices, crossed(): return lax.ppermute(v, axis, [(i, i ^ mask) for i in range(SIZES[axis])])  16.4 us
    ppermute x1, starting transfers between devices, inverted(): moved_one = lax.ppermute(masked_one, ALL, owners())  9.32 us
    unnamed x77, local copies, waits for them, and re-layouts  5.6 us
  transfers between devices with their start and end apart: 40, of which 18 were waited for; matrix products, arithmetic and copies ran while one was open for 1% of the time, Pallas kernels for 10%

profile of v3, /device:TPU:1, one launch (start us, length us, event | category | flops | bytes accessed | tf_op | source)
XLA Modules:
  0.0 223.7 jit_solution(15676355927030132508)
XLA Ops:
  8.3 9.3 %collective-permute-start = (f32[48,512]{1,0:T(8,128)}, f32[48,512]{1,0:T(8,128)S(1)}, u32[]{:S(2)}, u32[]{:S(2)}) collective-permute-start(f32[48,512]{1,0:T(8,128)} %get-tuple-element.54), channel_id=1, source_target_pairs={{0,176},{1,48},{2,184},{3,56},{4,112},{5,240},{6,120},{7,248},{8,1... | collective-permute-start | bytes 294920 | tf_op jit(solution)/shard_map/ppermute | solution.py:338
  17.6 3.5 %collective-permute-start.1 = (f32[48,512]{1,0:T(8,128)}, f32[48,512]{1,0:T(8,128)S(1)}, u32[]{:S(2)}, u32[]{:S(2)}) collective-permute-start(f32[48,512]{1,0:T(8,128)} %get-tuple-element.55), channel_id=1, source_target_pairs={{0,176},{1,48},{2,184},{3,56},{4,112},{5,240},{6,120},{7,248},{8,1... | collective-permute-start | bytes 294920 | tf_op jit(solution)/shard_map/ppermute | solution.py:337
  21.2 3.4 %shard_map.120 = (bf16[384,1536]{1,0:T(8,128)(2,1)}, bf16[384,1536]{1,0:T(8,128)(2,1)}) custom-call(f32[384,1536]{1,0:T(8,128)} %a.1), custom_call_target="tpu_custom_call" | custom-call | tf_op jit(solution)/shard_map/pallas_call | solution.py:20
  27.4 5.1 %collective-permute-start.5 = (f32[48,512]{1,0:T(8,128)S(1)}, f32[48,512]{1,0:T(8,128)S(1)}, u32[]{:S(2)}, u32[]{:S(2)}) collective-permute-start(f32[48,512]{1,0:T(8,128)S(1)} %collective-permute-done.refs_0_), channel_id=1, source_target_pairs={{0,64},{64,128},{128,192},{192,0},{1,65},{65,129},{129,193},{193,1... | collective-permute-start | bytes 294920 | tf_op jit(solution)/shard_map/ppermute | solution.py:47
  45.5 5.4 %collective-permute-done.12.refs_3_ = f32[192,512]{1,0:T(8,128)S(1)} collective-permute-done((f32[192,512]{1,0:T(8,128)}, f32[192,512]{1,0:T(8,128)S(1)}, u32[]{:S(2)}, u32[]{:S(2)}) %collective-permute-start.12) | collective-permute-done | bytes 393248 | tf_op jit(solution)/shard_map/ppermute | solution.py:47
  53.6 7.8 %collective-permute-done.20.refs_3_ = f32[48,512]{1,0:T(8,128)S(1)} collective-permute-done((f32[48,512]{1,0:T(8,128)S(1)}, f32[48,512]{1,0:T(8,128)S(1)}, u32[]{:S(2)}, u32[]{:S(2)}) %collective-permute-start.20) | collective-permute-done | bytes 98336 | tf_op jit(solution)/shard_map/ppermute | solution.py:47
  61.4 6.0 %collective-permute-done.21.refs_4_ = f32[48,512]{1,0:T(8,128)S(1)} collective-permute-done((f32[48,512]{1,0:T(8,128)S(1)}, f32[48,512]{1,0:T(8,128)S(1)}, u32[]{:S(2)}, u32[]{:S(2)}) %collective-permute-start.21) | collective-permute-done | bytes 98336 | tf_op jit(solution)/shard_map/ppermute | solution.py:47
  79.2 5.0 %collective-permute-done.23.refs_4_ = f32[192,512]{1,0:T(8,128)S(1)} collective-permute-done((f32[192,512]{1,0:T(8,128)}, f32[192,512]{1,0:T(8,128)S(1)}, u32[]{:S(2)}, u32[]{:S(2)}) %collective-permute-start.23) | collective-permute-done | bytes 393248 | tf_op jit(solution)/shard_map/ppermute | solution.py:47
  87.8 5.0 %collective-permute-done.27.refs_8_ = f32[192,512]{1,0:T(8,128)S(1)} collective-permute-done((f32[192,512]{1,0:T(8,128)S(1)}, f32[192,512]{1,0:T(8,128)S(1)}, u32[]{:S(2)}, u32[]{:S(2)}) %collective-permute-start.27) | collective-permute-done | bytes 393248 | tf_op jit(solution)/shard_map/ppermute | solution.py:47
  96.1 6.0 %shard_map.124 = (f32[192,512]{1,0:T(8,128)}, f32[192,512]{1,0:T(8,128)}) custom-call(bf16[384,1536]{1,0:T(8,128)(2,1)} %get-tuple-element.59.refs_0_, bf16[384,1536]{1,0:T(8,128)(2,1)} %get-tuple-element.60.refs_1_, f32[192,512]{1,0:T(8,128)} %get-tuple-element.73.refs_2_, f32[192,512]{1,0:T(8,128)} %get-tuple-element.74.refs_3_, f32[192,512]{1,0:T(8,128)} %copy-done.13, ...), custom_call_target="tpu_custom_call" | custom-call | tf_op jit(solution)/shard_map/pallas_call | solution.py:20
  102.1 9.4 %collective-permute-start.29 = (f32[192,512]{1,0:T(8,128)}, f32[192,512]{1,0:T(8,128)S(1)}, u32[]{:S(2)}, u32[]{:S(2)}) collective-permute-start(f32[192,512]{1,0:T(8,128)} %get-tuple-element.76), channel_id=1, source_target_pairs={{0,1},{1,0},{2,3},{3,2},{4,5},{5,4},{6,7},{7,6},{8,9},{9,8},{10,11... | collective-permute-start | bytes 1179656 | tf_op jit(solution)/shard_map/ppermute | solution.py:51
  112.4 5.9 %shard_map.122 = (f32[192,512]{1,0:T(8,128)}, f32[192,512]{1,0:T(8,128)}) custom-call(bf16[384,1536]{1,0:T(8,128)(2,1)} %get-tuple-element.59.refs_0_, bf16[384,1536]{1,0:T(8,128)(2,1)} %get-tuple-element.60.refs_1_, f32[192,512]{1,0:T(8,128)} %shard_map.121.refs_2_, f32[192,512]{1,0:T(8,128)} %copy-done.6, f32[192,512]{1,0:T(8,128)} %copy-done.7, ...), custom_call_target="tpu_custom_call" | custom-call | tf_op jit(solution)/shard_map/pallas_call | solution.py:20
  126.1 3.0 %collective-permute-done.30.t = f32[96,256]{1,0:T(8,128)S(1)} collective-permute-done((f32[96,256]{1,0:T(8,128)}, f32[96,256]{1,0:T(8,128)S(1)}, u32[]{:S(2)}, u32[]{:S(2)}) %collective-permute-start.30) | collective-permute-done | bytes 98336 | tf_op jit(solution)/shard_map/ppermute | solution.py:47
  129.0 3.8 %collective-permute-done.31.b = f32[96,256]{1,0:T(8,128)S(1)} collective-permute-done((f32[96,256]{1,0:T(8,128)}, f32[96,256]{1,0:T(8,128)S(1)}, u32[]{:S(2)}, u32[]{:S(2)}) %collective-permute-start.31) | collective-permute-done | bytes 98336 | tf_op jit(solution)/shard_map/ppermute | solution.py:47
  138.1 4.2 %collective-permute-done.32.b = f32[192,256]{1,0:T(8,128)S(1)} collective-permute-done((f32[192,256]{1,0:T(8,128)}, f32[192,256]{1,0:T(8,128)S(1)}, u32[]{:S(2)}, u32[]{:S(2)}) %collective-permute-start.32) | collective-permute-done | bytes 196640 | tf_op jit(solution)/shard_map/ppermute | solution.py:47
  143.1 3.3 %shard_map.127 = (f32[192,256]{1,0:T(8,128)}, f32[768,128]{1,0:T(8,128)}, f32[768,128]{1,0:T(8,128)}) custom-call(f32[192,256]{1,0:T(8,128)} %get-tuple-element.77.a, f32[192,256]{1,0:T(8,128)} %copy-done.20, f32[192,256]{1,0:T(8,128)} %copy-done.21, f32[48,1024]{1,0:T(8,128)} %get-tuple-element.84.refs_0_, f32[48,1024]{1,0:T(8,128)} %copy-done.17, ...), custom_call_target="tpu_custom_call" | custom-call | tf_op jit(solution)/shard_map/pallas_call | solution.py:20
  150.9 10.2 %all_to_all.15 = f32[4,192,128]{2,1,0:T(8,128)S(1)} all-to-all(f32[4,192,128]{2,1,0:T(8,128)S(1)} %bitcast.16), channel_id=1, replica_groups=mesh['x'=4,'z'=8,'y'=4,'k'=2] {'x'}, dimensions={0} | all-to-all | bytes 786432 | tf_op jit(solution)/shard_map/all_to_all | solution.py:55
  161.2 3.9 %all-to-all-start.1 = ((f32[4,48,256]{2,1,0:T(8,128)}), f32[4,48,256]{2,1,0:T(8,128)S(1)}, u32[]{:S(2)}, u32[]{:S(2)}) async-start(f32[4,48,256]{2,1,0:T(8,128)} %bitcast.3), calls=%async_computation.1 | async-start | bytes 393216 | tf_op jit(solution)/shard_map/all_to_all | solution.py:55
  165.0 5.8 %shard_map.128 = (f32[512,512]{1,0:T(8,128)}, f32[512,512]{1,0:T(8,128)}) custom-call(f32[512,512]{1,0:T(8,128)} %one.3, f32[512,512]{1,0:T(8,128)} %two.3), custom_call_target="tpu_custom_call" | custom-call | tf_op jit(solution)/shard_map/pallas_call | solution.py:20
  171.0 4.4 %collective-permute-done.36 = f32[192,128]{1,0:T(8,128)S(1)} collective-permute-done((f32[192,128]{1,0:T(8,128)S(1)}, f32[192,128]{1,0:T(8,128)S(1)}, u32[]{:S(2)}, u32[]{:S(2)}) %collective-permute-start.36) | collective-permute-done | bytes 98336 | tf_op jit(solution)/shard_map/ppermute | solution.py:51
  176.0 6.9 %collective-permute-done.37 = f32[192,128]{1,0:T(8,128)S(1)} collective-permute-done((f32[192,128]{1,0:T(8,128)S(1)}, f32[192,128]{1,0:T(8,128)S(1)}, u32[]{:S(2)}, u32[]{:S(2)}) %collective-permute-start.37) | collective-permute-done | bytes 98336 | tf_op jit(solution)/shard_map/ppermute | solution.py:51
  183.1 22.3 %all_to_all.16.own = f32[16,192,128]{2,1,0:T(8,128)S(1)} all-to-all(f32[16,192,128]{2,1,0:T(8,128)S(1)} %broadcast_in_dim.11), channel_id=1, replica_groups=mesh['x'=4,'z'=8,'y'=4,'k'=2] {'x','y'}, dimensions={0} | all-to-all | bytes 3145728 | tf_op jit(solution)/shard_map/all_to_all | solution.py:55
  205.3 6.3 %collective-permute-start.38 = (f32[16,192,128]{2,1,0:T(8,128)S(1)}, f32[16,192,128]{2,1,0:T(8,128)S(1)}, u32[]{:S(2)}, u32[]{:S(2)}) collective-permute-start(f32[16,192,128]{2,1,0:T(8,128)S(1)} %all_to_all.16.own), channel_id=1, source_target_pairs={{0,1},{1,0},{2,3},{3,2},{4,5},{5,4},{6,7},{7,6},{8,9},{9,8},{10,11... | collective-permute-start | bytes 4718600 | tf_op jit(solution)/shard_map/ppermute | solution.py:51
  215.8 7.9 %shard_map.129 = (f32[512,512]{1,0:T(8,128)}, f32[512,512]{1,0:T(8,128)}, f32[512,512]{1,0:T(8,128)}) custom-call(f32[16,192,128]{2,1,0:T(8,128)} %copy-done, f32[16,192,128]{2,1,0:T(8,128)} %copy-done.2, f32[512,512]{1,0:T(8,128)} %get-tuple-element.95.g1, f32[512,512]{1,0:T(8,128)} %get-tuple-element.96.g2, f32[512,512]{1,0:T(8,128)} %u_ref.1), custom_call_target="tpu_custom_call" | custom-call | tf_op jit(solution)/shard_map/pallas_call | solution.py:20
  (155 shorter events, 68.7 us)
Async XLA Ops:
  2.5 22.1 %collective-permute-start.2 = (f32[48,1024]{1,0:T(8,128)}, f32[48,1024]{1,0:T(8,128)S(1)}, u32[]{:S(2)}, u32[]{:S(2)}) collective-permute-start(f32[48,1024]{1,0:T(8,128)} %get-tuple-element.84.refs_0_), channel_id=1, source_target_pairs={{0,2},{2,4},{4,6},{6,0},{1,3},{3,5},{5,7},{7,1},{8,10},{10,12},{12... | collective-permute-start | bytes 589832 | tf_op jit(solution)/shard_map/ppermute | solution.py:47
  4.6 20.0 %collective-permute-start.3 = (f32[48,1024]{1,0:T(8,128)}, f32[48,1024]{1,0:T(8,128)S(1)}, u32[]{:S(2)}, u32[]{:S(2)}) collective-permute-start(f32[48,1024]{1,0:T(8,128)} %get-tuple-element.84.refs_0_), channel_id=1, source_target_pairs={{0,4},{2,6},{4,0},{6,2},{1,5},{3,7},{5,1},{7,3},{8,12},{10,14},{12... | collective-permute-start | bytes 589832 | tf_op jit(solution)/shard_map/ppermute | solution.py:47
  7.2 17.4 %collective-permute-start.4 = (f32[48,1024]{1,0:T(8,128)}, f32[48,1024]{1,0:T(8,128)S(1)}, u32[]{:S(2)}, u32[]{:S(2)}) collective-permute-start(f32[48,1024]{1,0:T(8,128)} %get-tuple-element.84.refs_0_), channel_id=1, source_target_pairs={{0,6},{2,0},{4,2},{6,4},{1,7},{3,1},{5,3},{7,5},{8,14},{10,8},{12,... | collective-permute-start | bytes 589832 | tf_op jit(solution)/shard_map/ppermute | solution.py:47
  8.3 16.3 %collective-permute-start = (f32[48,512]{1,0:T(8,128)}, f32[48,512]{1,0:T(8,128)S(1)}, u32[]{:S(2)}, u32[]{:S(2)}) collective-permute-start(f32[48,512]{1,0:T(8,128)} %get-tuple-element.54), channel_id=1, source_target_pairs={{0,176},{1,48},{2,184},{3,56},{4,112},{5,240},{6,120},{7,248},{8,1... | collective-permute-start | bytes 294920 | tf_op jit(solution)/shard_map/ppermute | solution.py:338
  24.7 10.3 %collective-permute-start.10 = (f32[48,512]{1,0:T(8,128)S(1)}, f32[48,512]{1,0:T(8,128)S(1)}, u32[]{:S(2)}, u32[]{:S(2)}) collective-permute-start(f32[48,512]{1,0:T(8,128)S(1)} %collective-permute-done.1.refs_0_), channel_id=1, source_target_pairs={{0,56},{8,0},{16,8},{24,16},{32,24},{40,32},{48,40},{56,48},{1,57}... | collective-permute-start | bytes 294920 | tf_op jit(solution)/shard_map/ppermute | solution.py:47
  25.8 10.5 %collective-permute-start.8 = (f32[48,512]{1,0:T(8,128)S(1)}, f32[48,512]{1,0:T(8,128)S(1)}, u32[]{:S(2)}, u32[]{:S(2)}) collective-permute-start(f32[48,512]{1,0:T(8,128)S(1)} %collective-permute-done.1.refs_0_), channel_id=1, source_target_pairs={{0,8},{8,16},{16,24},{24,32},{32,40},{40,48},{48,56},{56,0},{1,9},... | collective-permute-start | bytes 294920 | tf_op jit(solution)/shard_map/ppermute | solution.py:47
  27.4 9.0 %collective-permute-start.5 = (f32[48,512]{1,0:T(8,128)S(1)}, f32[48,512]{1,0:T(8,128)S(1)}, u32[]{:S(2)}, u32[]{:S(2)}) collective-permute-start(f32[48,512]{1,0:T(8,128)S(1)} %collective-permute-done.refs_0_), channel_id=1, source_target_pairs={{0,64},{64,128},{128,192},{192,0},{1,65},{65,129},{129,193},{193,1... | collective-permute-start | bytes 294920 | tf_op jit(solution)/shard_map/ppermute | solution.py:47
  42.8 30.1 %collective-permute-start.13 = (f32[192,512]{1,0:T(8,128)}, f32[192,512]{1,0:T(8,128)S(1)}, u32[]{:S(2)}, u32[]{:S(2)}) collective-permute-start(f32[192,512]{1,0:T(8,128)} %shard_map.121.refs_2_), channel_id=1, source_target_pairs={{0,56},{8,0},{16,8},{24,16},{32,24},{40,32},{48,40},{56,48},{1,57}... | collective-permute-start | bytes 1179656 | tf_op jit(solution)/shard_map/ppermute | solution.py:47
  50.9 22.1 %collective-permute-start.14 = (f32[192,512]{1,0:T(8,128)S(1)}, f32[192,512]{1,0:T(8,128)S(1)}, u32[]{:S(2)}, u32[]{:S(2)}) collective-permute-start(f32[192,512]{1,0:T(8,128)S(1)} %collective-permute-done.12.refs_3_), channel_id=1, source_target_pairs={{0,8},{8,16},{16,24},{24,32},{32,40},{40,48},{48,56},{56,0},{1,9},... | collective-permute-start | bytes 1179656 | tf_op jit(solution)/shard_map/ppermute | solution.py:47
  50.9 10.5 %collective-permute-start.20 = (f32[48,512]{1,0:T(8,128)S(1)}, f32[48,512]{1,0:T(8,128)S(1)}, u32[]{:S(2)}, u32[]{:S(2)}) collective-permute-start(f32[48,512]{1,0:T(8,128)S(1)} %collective-permute-done.9.refs_2_), channel_id=1, source_target_pairs={{0,8},{8,16},{16,24},{24,32},{32,40},{40,48},{48,56},{56,0},{1,9},... | collective-permute-start | bytes 294920 | tf_op jit(solution)/shard_map/ppermute | solution.py:47
  50.9 10.5 %collective-permute-start.22 = (f32[48,512]{1,0:T(8,128)S(1)}, f32[48,512]{1,0:T(8,128)S(1)}, u32[]{:S(2)}, u32[]{:S(2)}) collective-permute-start(f32[48,512]{1,0:T(8,128)S(1)} %collective-permute-done.11.refs_6_), channel_id=1, source_target_pairs={{0,56},{8,0},{16,8},{24,16},{32,24},{40,32},{48,40},{56,48},{1,57}... | collective-permute-start | bytes 294920 | tf_op jit(solution)/shard_map/ppermute | solution.py:47
  71.9 12.4 %collective-permute-start.23 = (f32[192,512]{1,0:T(8,128)}, f32[192,512]{1,0:T(8,128)S(1)}, u32[]{:S(2)}, u32[]{:S(2)}) collective-permute-start(f32[192,512]{1,0:T(8,128)} %get-tuple-element.73.refs_2_), channel_id=1, source_target_pairs={{0,64},{64,128},{128,192},{192,0},{1,65},{65,129},{129,193},{193,1... | collective-permute-start | bytes 1179656 | tf_op jit(solution)/shard_map/ppermute | solution.py:47
  73.0 11.3 %collective-permute-start.15 = (f32[192,512]{1,0:T(8,128)S(1)}, f32[192,512]{1,0:T(8,128)S(1)}, u32[]{:S(2)}, u32[]{:S(2)}) collective-permute-start(f32[192,512]{1,0:T(8,128)S(1)} %collective-permute-done.13.refs_4_), channel_id=1, source_target_pairs={{0,56},{8,0},{16,8},{24,16},{32,24},{40,32},{48,40},{56,48},{1,57}... | collective-permute-start | bytes 1179656 | tf_op jit(solution)/shard_map/ppermute | solution.py:47
  73.0 11.4 %collective-permute-start.16 = (f32[192,512]{1,0:T(8,128)S(1)}, f32[192,512]{1,0:T(8,128)S(1)}, u32[]{:S(2)}, u32[]{:S(2)}) collective-permute-start(f32[192,512]{1,0:T(8,128)S(1)} %collective-permute-done.14.refs_5_), channel_id=1, source_target_pairs={{0,8},{8,16},{16,24},{24,32},{32,40},{40,48},{48,56},{56,0},{1,9},... | collective-permute-start | bytes 1179656 | tf_op jit(solution)/shard_map/ppermute | solution.py:47
  77.3 10.5 %collective-permute-start.26 = (f32[192,512]{1,0:T(8,128)}, f32[192,512]{1,0:T(8,128)S(1)}, u32[]{:S(2)}, u32[]{:S(2)}) collective-permute-start(f32[192,512]{1,0:T(8,128)} %get-tuple-element.74.refs_3_), channel_id=1, source_target_pairs={{0,192},{64,0},{128,64},{192,128},{1,193},{65,1},{129,65},{193,129... | collective-permute-start | bytes 1179656 | tf_op jit(solution)/shard_map/ppermute | solution.py:47
  79.2 13.7 %collective-permute-start.27 = (f32[192,512]{1,0:T(8,128)S(1)}, f32[192,512]{1,0:T(8,128)S(1)}, u32[]{:S(2)}, u32[]{:S(2)}) collective-permute-start(f32[192,512]{1,0:T(8,128)S(1)} %collective-permute-done.25.refs_6_), channel_id=1, source_target_pairs={{0,192},{64,0},{128,64},{192,128},{1,193},{65,1},{129,65},{193,129... | collective-permute-start | bytes 1179656 | tf_op jit(solution)/shard_map/ppermute | solution.py:47
  84.3 11.8 %collective-permute-start.28 = (f32[192,512]{1,0:T(8,128)S(1)}, f32[192,512]{1,0:T(8,128)}, u32[]{:S(2)}, u32[]{:S(2)}) collective-permute-start(f32[192,512]{1,0:T(8,128)S(1)} %collective-permute-done.24.refs_5_), channel_id=1, source_target_pairs={{0,64},{64,128},{128,192},{192,0},{1,65},{65,129},{129,193},{193,1... | collective-permute-start | bytes 1179656 | tf_op jit(solution)/shard_map/ppermute | solution.py:47
  84.3 27.3 %collective-permute-start.17 = (f32[192,512]{1,0:T(8,128)S(1)}, f32[192,512]{1,0:T(8,128)S(1)}, u32[]{:S(2)}, u32[]{:S(2)}) collective-permute-start(f32[192,512]{1,0:T(8,128)S(1)} %collective-permute-done.15.refs_6_), channel_id=1, source_target_pairs={{0,56},{8,0},{16,8},{24,16},{32,24},{40,32},{48,40},{56,48},{1,57}... | collective-permute-start | bytes 1179656 | tf_op jit(solution)/shard_map/ppermute | solution.py:47
  84.4 27.2 %collective-permute-start.18 = (f32[192,512]{1,0:T(8,128)S(1)}, f32[192,512]{1,0:T(8,128)}, u32[]{:S(2)}, u32[]{:S(2)}) collective-permute-start(f32[192,512]{1,0:T(8,128)S(1)} %collective-permute-done.16.refs_7_), channel_id=1, source_target_pairs={{0,8},{8,16},{16,24},{24,32},{32,40},{40,48},{48,56},{56,0},{1,9},... | collective-permute-start | bytes 1179656 | tf_op jit(solution)/shard_map/ppermute | solution.py:47
  102.1 16.2 %collective-permute-start.29 = (f32[192,512]{1,0:T(8,128)}, f32[192,512]{1,0:T(8,128)S(1)}, u32[]{:S(2)}, u32[]{:S(2)}) collective-permute-start(f32[192,512]{1,0:T(8,128)} %get-tuple-element.76), channel_id=1, source_target_pairs={{0,1},{1,0},{2,3},{3,2},{4,5},{5,4},{6,7},{7,6},{8,9},{9,8},{10,11... | collective-permute-start | bytes 1179656 | tf_op jit(solution)/shard_map/ppermute | solution.py:51
  123.4 9.5 %collective-permute-start.31 = (f32[96,256]{1,0:T(8,128)}, f32[96,256]{1,0:T(8,128)S(1)}, u32[]{:S(2)}, u32[]{:S(2)}) collective-permute-start(f32[96,256]{1,0:T(8,128)} %get-tuple-element.81), channel_id=1, source_target_pairs={{0,6},{2,0},{4,2},{6,4},{1,7},{3,1},{5,3},{7,5},{8,14},{10,8},{12,... | collective-permute-start | bytes 294920 | tf_op jit(solution)/shard_map/ppermute | solution.py:47
  161.1 9.8 %collective-permute-start.35 = (f32[192,128]{1,0:T(8,128)S(1)}, f32[192,128]{1,0:T(8,128)S(1)}, u32[]{:S(2)}, u32[]{:S(2)}) collective-permute-start(f32[192,128]{1,0:T(8,128)S(1)} %reduce_sum.9), channel_id=1, source_target_pairs={{0,8},{8,0},{16,24},{24,16},{32,40},{40,32},{48,56},{56,48},{1,9},... | collective-permute-start | bytes 294920 | tf_op jit(solution)/shard_map/ppermute | solution.py:51
  161.2 14.2 %all-to-all-start.1 = ((f32[4,48,256]{2,1,0:T(8,128)}), f32[4,48,256]{2,1,0:T(8,128)S(1)}, u32[]{:S(2)}, u32[]{:S(2)}) async-start(f32[4,48,256]{2,1,0:T(8,128)} %bitcast.3), calls=%async_computation.1 | async-start | bytes 393216 | tf_op jit(solution)/shard_map/all_to_all | solution.py:55
  205.3 9.3 %collective-permute-start.38 = (f32[16,192,128]{2,1,0:T(8,128)S(1)}, f32[16,192,128]{2,1,0:T(8,128)S(1)}, u32[]{:S(2)}, u32[]{:S(2)}) collective-permute-start(f32[16,192,128]{2,1,0:T(8,128)S(1)} %all_to_all.16.own), channel_id=1, source_target_pairs={{0,1},{1,0},{2,3},{3,2},{4,5},{5,4},{6,7},{7,6},{8,9},{9,8},{10,11... | collective-permute-start | bytes 4718600 | tf_op jit(solution)/shard_map/ppermute | solution.py:51
  (54 other events, 715.2 us)
